TPU v7x, 512 devices: a whole 4x8x8 slice. The times are simulated.
512 devices in a mesh: band: 32 (over y, x_hi, core), samp: 16 (over z, x_lo).
Axes of the slice: x: 4 (x_hi: 2, x_lo: 2; x = x_hi * 2 + x_lo), y: 8, z: 8, core: 2. Of those that a mesh axis runs over, the one named last changes fastest.
Arguments:
- dosage: bfloat16 [32768, 16384], P('samp', 'band'), may hold values from -1 to 2, as said below
Outputs:
- linkage: float32 [16384, 2048], P(('band', 'samp'))
Inputs may be any that keep to these rules, and one draw needn't show every extreme that they name: -1 marks a missing call; every other entry is an imputed dosage between 0 and 2.
All inputs are finite; a program needn't handle non-finite values.
Results may differ from a plain program's by a relative error of at most 0.0015.
Values may be sent and summed in bfloat16 or wider, within the bound.
No kernel may reach another device: no remote copies, remote signals or barrier semaphores. Data moves between devices by JAX's collectives and lax.ppermute only.
A program may use at most 64 MiB of HBM per device.

v0:
```python
import jax
import jax.numpy as jnp
from jax import lax
from jax.sharding import PartitionSpec as P

TILE = 512
WIN = 2048


def sent_to_all(value, axis):
    copies = jnp.broadcast_to(value, (lax.axis_size(axis), *value.shape))
    return lax.all_to_all(copies, axis, split_axis=0, concat_axis=0, tiled=True)


def of_everyone(value, axis):
    everything = sent_to_all(value, axis)
    return jnp.sum(everything, axis=0)


def together(arrays, axis):
    ends = [0]
    for a in arrays:
        ends.append(ends[-1] + a.size)
    subtotal = of_everyone(jnp.concatenate([a.ravel() for a in arrays]), axis)
    return tuple((subtotal[b:e].reshape(a.shape) for a, b, e in zip(arrays, ends, ends[1:])))


def passed_along(value, axis, steps):
    count = lax.axis_size(axis)
    leading, last = (max(0, -steps), min(count, count - steps))
    return lax.ppermute(value, axis, [(source, source + steps) for source in range(leading, last)])


def in_blocks(value, dim, peers):
    before, after = (value.shape[:dim], value.shape[dim + 1 :])
    return jnp.moveaxis(value.reshape(*before, peers, -1, *after), dim, 0)


def sent_and_summed(value, axis, dim):
    parts = in_blocks(value, dim, lax.axis_size(axis))
    arrived = lax.all_to_all(parts, axis, split_axis=0, concat_axis=0, tiled=True)
    return arrived.astype(jnp.float32).sum(axis=0)


def on_device(dosage):
    raw = dosage.astype(jnp.float32)
    observed = (raw >= 0.0).astype(jnp.float32)
    values = observed * raw
    count, total, square = together(
        (jnp.sum(observed, axis=0), jnp.sum(values, axis=0), jnp.sum(values * values, axis=0)),
        "samp",
    )
    samples = dosage.shape[0] * lax.axis_size("samp")
    mean = (total + 1.0) / (count + 1.0)
    spread = (square - 2.0 * mean * total + count * mean * mean + 0.5) / (count + 1.0)
    scaled = (observed * (values - mean) * lax.rsqrt(spread)).astype(jnp.bfloat16)
    band_width = scaled.shape[1]
    reach = (WIN - TILE + band_width - 1) // band_width
    panels = [scaled]
    for step in range(1, reach + 1):
        panels.append(passed_along(scaled, "band", -step))
    window = jnp.concatenate(panels, axis=1)
    product = lax.dot_general(
        scaled, window, (((0,), (0,)), ((), ())), preferred_element_type=jnp.float32
    )
    return sent_and_summed((product / samples).astype(jnp.bfloat16), "samp", 0)


def solution(mesh):
    return jax.shard_map(
        on_device,
        mesh=mesh,
        in_specs=(P("samp", "band"),),
        out_specs=P(("band", "samp"), None),
        check_vma=False,
    )
```

profile of v0, /device:TPU:7, one launch (start us, length us, event | category | flops | bytes accessed | tf_op | source)
XLA Modules:
  0.0 200.2 jit_solution(13421793278536118456)
XLA Ops:
  0.0 0.0 copy-start
  0.0 2.8 %fusion.13 = (f32[512]{0:T(512)S(1)}, f32[512]{0:T(512)S(1)}, f32[512]{0:T(512)S(1)}) fusion(bf16[2048,512]{1,0:T(8,128)(2,1)} %param.1), kind=kLoop, calls=%fused_computation.15 | loop fusion | flops 8387072 | bytes 2103296 | tf_op jit(solution)/shard_map/reduce_sum | solution.py:50
  2.9 0.1 broadcast_in_dim.2
  2.9 18.3 %all_to_all.11 = f32[16,1,1536]{2,1,0:T(1,128)S(1)} all-to-all(f32[16,1,1536]{2,1,0:T(1,128)S(1)} %broadcast_in_dim.2), channel_id=1, replica_groups=mesh['band'=32,'samp'=16] {'samp'}, dimensions={0} | all-to-all | bytes 196608 | tf_op jit(solution)/shard_map/all_to_all | solution.py:12
  21.2 0.1 reduce_sum.48
  21.3 0.0 copy-done
  21.3 0.9 fusion.15
  22.2 5.0 %collective-permute-start.2 = (bf16[2048,512]{1,0:T(8,128)(2,1)S(1)}, bf16[2048,512]{1,0:T(8,128)(2,1)S(1)}, u32[]{:S(2)}, u32[]{:S(2)}) collective-permute-start(bf16[2048,512]{1,0:T(8,128)(2,1)S(1)} %fusion.15), channel_id=1, source_target_pairs={{48,0},{64,16},{80,32},{96,48},{112,64},{128,80},{144,96},{160,112... | collective-permute-start | bytes 6291464 | tf_op jit(solution)/shard_map/ppermute | solution.py:31
  27.2 1.9 collective-permute-start.1
  29.1 1.9 collective-permute-start
  31.1 39.7 %collective-permute-done.2 = bf16[2048,512]{1,0:T(8,128)(2,1)S(1)} collective-permute-done((bf16[2048,512]{1,0:T(8,128)(2,1)S(1)}, bf16[2048,512]{1,0:T(8,128)(2,1)S(1)}, u32[]{:S(2)}, u32[]{:S(2)}) %collective-permute-start.2) | collective-permute-done | bytes 2097184 | tf_op jit(solution)/shard_map/ppermute | solution.py:31
  70.8 59.9 %collective-permute-done.1 = bf16[2048,512]{1,0:T(8,128)(2,1)S(1)} collective-permute-done((bf16[2048,512]{1,0:T(8,128)(2,1)S(1)}, bf16[2048,512]{1,0:T(8,128)(2,1)S(1)}, u32[]{:S(2)}, u32[]{:S(2)}) %collective-permute-start.1) | collective-permute-done | bytes 2097184 | tf_op jit(solution)/shard_map/ppermute | solution.py:31
  130.7 31.1 %collective-permute-done = bf16[2048,512]{1,0:T(8,128)(2,1)S(1)} collective-permute-done((bf16[2048,512]{1,0:T(8,128)(2,1)S(1)}, bf16[2048,512]{1,0:T(8,128)(2,1)S(1)}, u32[]{:S(2)}, u32[]{:S(2)}) %collective-permute-start) | collective-permute-done | bytes 2097184 | tf_op jit(solution)/shard_map/ppermute | solution.py:31
  161.8 6.0 %multiply_convert_fusion = bf16[512,2048]{1,0:T(8,128)(2,1)S(1)} fusion(bf16[2048,512]{1,0:T(8,128)(2,1)S(1)} %fusion.15, bf16[2048,512]{1,0:T(8,128)(2,1)S(1)} %collective-permute-done.2, bf16[2048,512]{1,0:T(8,128)(2,1)S(1)} %collective-permute-done.1, bf16[2048,512]{1,0:T(8,128)(2,1)S(1)} %collective-permute-done), kind=kOutput, calls=%fused_computation.20 | convolution fusion | flops 4330618880 | bytes 10485760 | tf_op jit(solution)/shard_map/dot_general | solution.py:63
  167.8 31.3 %all_to_all.12 = bf16[16,32,2048]{2,1,0:T(8,128)(2,1)S(1)} all-to-all(bf16[16,32,2048]{2,1,0:T(8,128)(2,1)S(1)} %bitcast.2), channel_id=1, replica_groups=mesh['band'=32,'samp'=16] {'samp'}, dimensions={0} | all-to-all | bytes 4194304 | tf_op jit(solution)/shard_map/all_to_all | solution.py:41
  199.1 1.1 convert_reduce_fusion
  (2 shorter events, 0.0 us)
Async XLA Ops:
  0.0 21.3 %copy-start = (bf16[2048,512]{1,0:T(8,128)(2,1)S(1)}, bf16[2048,512]{1,0:T(8,128)(2,1)}, u32[]{:S(2)}) copy-start(bf16[2048,512]{1,0:T(8,128)(2,1)} %param.1) | copy-start | bytes 6291460
  22.2 48.6 %collective-permute-start.2 = (bf16[2048,512]{1,0:T(8,128)(2,1)S(1)}, bf16[2048,512]{1,0:T(8,128)(2,1)S(1)}, u32[]{:S(2)}, u32[]{:S(2)}) collective-permute-start(bf16[2048,512]{1,0:T(8,128)(2,1)S(1)} %fusion.15), channel_id=1, source_target_pairs={{48,0},{64,16},{80,32},{96,48},{112,64},{128,80},{144,96},{160,112... | collective-permute-start | bytes 6291464 | tf_op jit(solution)/shard_map/ppermute | solution.py:31
  27.2 103.5 %collective-permute-start.1 = (bf16[2048,512]{1,0:T(8,128)(2,1)S(1)}, bf16[2048,512]{1,0:T(8,128)(2,1)S(1)}, u32[]{:S(2)}, u32[]{:S(2)}) collective-permute-start(bf16[2048,512]{1,0:T(8,128)(2,1)S(1)} %fusion.15), channel_id=1, source_target_pairs={{32,0},{48,16},{64,32},{80,48},{96,64},{112,80},{128,96},{144,112}... | collective-permute-start | bytes 6291464 | tf_op jit(solution)/shard_map/ppermute | solution.py:31
  29.1 132.7 %collective-permute-start = (bf16[2048,512]{1,0:T(8,128)(2,1)S(1)}, bf16[2048,512]{1,0:T(8,128)(2,1)S(1)}, u32[]{:S(2)}, u32[]{:S(2)}) collective-permute-start(bf16[2048,512]{1,0:T(8,128)(2,1)S(1)} %fusion.15), channel_id=1, source_target_pairs={{16,0},{32,16},{48,32},{64,48},{80,64},{96,80},{112,96},{128,112},... | collective-permute-start | bytes 6291464 | tf_op jit(solution)/shard_map/ppermute | solution.py:31
where the time goes:
time: 200 us
  waiting for transfers between devices  131 us (66%)
  blocking collectives  49.6 us (25%)
  starting transfers between devices  8.86 us (4%)
  matrix products  6 us (3%)
  other arithmetic  4.92 us (2%)
    ppermute x3, waiting for transfers between devices, passed_along(): lax.ppermute(value, axis, [(source, source + steps) for source in range(l...  131 us
    all_to_all x1, blocking collectives, sent_and_summed(): lax.all_to_all(parts, axis, split_axis=0, concat_axis=0, tiled=True)  31.3 us
    all_to_all x1, blocking collectives, sent_to_all(): return lax.all_to_all(copies, axis, split_axis=0, concat_axis=0, tiled=True)  18.3 us
    ppermute x3, starting transfers between devices, passed_along(): lax.ppermute(value, axis, [(source, source + steps) for source in range(l...  8.86 us
    dot_general x1, matrix products, on_device(): lax.dot_general(scaled, window, (((0,), (0,)), ((), ())), preferred_eleme...  6 us
  transfers between devices with their start and end apart: 3, of which 3 were waited for; matrix products, arithmetic and copies ran while one was open for 0% of the time, Pallas kernels for 0%

commit v1 on v0

v1 whole, which is shorter than its diff:
```python
import jax
import jax.numpy as jnp
from jax import lax
from jax.sharding import PartitionSpec as P

TILE = 512
WIN = 2048
AXES = ("band", "samp")
YS, XS, ZS, CORES = 8, 4, 8, 2


def index_of(y, x, z, core):
    return ((y * 2 + x // 2) * CORES + core) * (ZS * 2) + z * 2 + x % 2


def pairs_of(target_of):
    pairs = []
    for y in range(YS):
        for x in range(XS):
            for z in range(ZS):
                for core in range(CORES):
                    target = target_of(y, x, z, core)
                    if target is not None and target[0] >= 0:
                        pairs.append((index_of(y, x, z, core), index_of(*target)))
    return pairs


NEXT_CHIP = pairs_of(lambda y, x, z, c: (y, x - 2, z, c) if x >= 2 else (y - 1, x + 2, z, c))
EDGE = pairs_of(lambda y, x, z, c: (y, x, z, 0) if c == 1 else (y - 1, x, z, 1))
OTHER_CORE = pairs_of(lambda y, x, z, c: (y, x, z, 1 - c))
OTHER_HALF = pairs_of(lambda y, x, z, c: (y, x ^ 1, z, c))
Z_GROUPS = [[low + 2 * z for z in range(ZS)] for low in range(2)]


def sent(value, pairs):
    return lax.ppermute(value, AXES, pairs)


def over_z(value):
    return lax.all_to_all(value, "samp", 0, 0, tiled=True, axis_index_groups=Z_GROUPS)


def standardized(raw, stats):
    raw = raw.astype(jnp.float32)
    observed = (raw >= 0.0).astype(jnp.float32)
    return (observed * (observed * raw - stats[0]) * stats[1]).astype(jnp.bfloat16)


def on_device(dosage):
    half = TILE // 2
    samples = dosage.shape[0] * lax.axis_size("samp")
    core = lax.axis_index("band") % 2
    low = lax.axis_index("samp") % 2

    edge_raw = sent(dosage, EDGE)
    raw = dosage.astype(jnp.float32)
    observed = (raw >= 0.0).astype(jnp.float32)
    values = observed * raw
    sums = jnp.stack([observed.sum(0), values.sum(0), (values * values).sum(0)])
    sums = sums + sent(sums, OTHER_HALF)
    first, sums = lax.optimization_barrier((dosage[:, :half], sums))
    next_raw = sent(first, NEXT_CHIP)
    everyone = over_z(jnp.broadcast_to(sums[None], (ZS, *sums.shape)))
    count, total, square = everyone.sum(0)
    mean = (total + 1.0) / (count + 1.0)
    spread = (square - 2.0 * mean * total + count * mean * mean + 0.5) / (count + 1.0)
    stats = jnp.stack([mean, lax.rsqrt(spread)])
    next_stats = sent(stats[:, :half], NEXT_CHIP)
    edge_stats = sent(stats, EDGE)
    scaled = standardized(dosage, stats)
    next_second = sent(scaled[:, half:], NEXT_CHIP)

    def tile(panel):
        product = lax.dot_general(
            scaled, panel, (((0,), (0,)), ((), ())), preferred_element_type=jnp.float32
        )
        product = (product / samples).astype(jnp.bfloat16)
        arrived = over_z(product.reshape(ZS, -1, product.shape[1]))
        return arrived.astype(jnp.float32).sum(0)

    def owned(rows):
        count = rows.shape[0] // 2
        mine = lax.dynamic_slice_in_dim(rows, low * count, count, 0)
        other = lax.dynamic_slice_in_dim(rows, (1 - low) * count, count, 0)
        return mine + sent(other, OTHER_HALF)

    own = tile(scaled)
    edge = tile(standardized(edge_raw, edge_stats))
    next_first = standardized(next_raw, next_stats)
    swapped_first = sent(next_first, OTHER_CORE)
    firsts = tile(jnp.concatenate([next_first, swapped_first], axis=1))
    swapped_second = sent(next_second, OTHER_CORE)
    seconds = tile(jnp.concatenate([next_second, swapped_second], axis=1))
    early = owned(jnp.concatenate([own, edge], axis=1))
    firsts = owned(firsts)
    seconds = owned(seconds)
    own, edge = early[:, :TILE], early[:, TILE:]
    nexts = jnp.concatenate([firsts[:, :half], seconds[:, :half]], axis=1)
    swaps = jnp.concatenate([firsts[:, half:], seconds[:, half:]], axis=1)
    even = core == 0
    return jnp.concatenate(
        [own, jnp.where(even, edge, swaps), nexts, jnp.where(even, swaps, edge)], axis=1
    )


def solution(mesh):
    return jax.shard_map(
        on_device,
        mesh=mesh,
        in_specs=(P("samp", "band"),),
        out_specs=P(("band", "samp"), None),
        check_vma=False,
    )
```

time: 200 us -> 179 us (0.90)
  the two profiles are of different devices: /device:TPU:7 before, /device:TPU:24 now
where the time goes in v1:
time: 179 us; the launch traced here: 177 us
  waiting for transfers between devices  83.7 us (47%)
  starting transfers between devices  65.7 us (37%)
  matrix products  13.1 us (7%)
  other arithmetic  9.97 us (6%)
  local copies, waits for them, and re-layouts  4.71 us (3%)
    ppermute x11, waiting for transfers between devices, sent(): return lax.ppermute(value, AXES, pairs)  45.2 us
    all_to_all x5, waiting for transfers between devices, over_z(): lax.all_to_all(value, 'samp', 0, 0, tiled=True, axis_index_groups=Z_GROUPS)  38.6 us
    ppermute x11, starting transfers between devices, sent(): return lax.ppermute(value, AXES, pairs)  35.1 us
    all_to_all x5, starting transfers between devices, over_z(): lax.all_to_all(value, 'samp', 0, 0, tiled=True, axis_index_groups=Z_GROUPS)  30.6 us
    dot_general x4, matrix products, tile(): lax.dot_general(scaled, panel, (((0,), (0,)), ((), ())), preferred_elemen...  13.1 us
    convert_element_type x2, other arithmetic, standardized(): (observed * (observed * raw - stats[0]) * stats[1]).astype(jnp.bfloat16)  5.15 us
  transfers between devices with their start and end apart: 16, of which 8 were waited for; matrix products, arithmetic and copies ran while one was open for 13% of the time, Pallas kernels for 0%

profile of v1, /device:TPU:24, one launch (start us, length us, event | category | flops | bytes accessed | tf_op | source)
XLA Modules:
  0.0 177.5 jit_solution(5765715430048181791)
XLA Ops:
  0.0 2.7 %fusion.5 = (f32[512]{0:T(512)S(1)}, f32[512]{0:T(512)S(1)}, f32[512]{0:T(512)S(1)}) fusion(bf16[2048,512]{1,0:T(8,128)(2,1)} %param.1), kind=kLoop, calls=%fused_computation.9 | loop fusion | flops 8387072 | bytes 2103296 | tf_op jit(solution)/shard_map/reduce_sum | solution.py:59
  2.7 3.4 %collective-permute-start = (f32[3,512]{1,0:T(4,128)S(1)}, f32[3,512]{1,0:T(4,128)S(1)}, u32[]{:S(2)}, u32[]{:S(2)}) collective-permute-start(f32[3,512]{1,0:T(4,128)S(1)} %pad_maximum_fusion.1), channel_id=1, source_target_pairs={{0,1},{16,17},{2,3},{18,19},{4,5},{20,21},{6,7},{22,23},{8,9},{24,... | collective-permute-start | bytes 18440 | tf_op jit(solution)/shard_map/ppermute | solution.py:36
  6.1 2.3 %slice.39 = bf16[2048,256]{1,0:T(8,128)(2,1)} slice(bf16[2048,512]{1,0:T(8,128)(2,1)} %param.1), slice={[0:2048], [0:256]} | slice | bytes 2097152 | tf_op jit(solution)/shard_map/slice | solution.py:61
  8.4 0.0 collective-permute-done
  8.4 0.6 broadcast_in_dim.2
  9.0 10.3 %all-to-all-start = ((f32[8,3,512]{2,1,0:T(4,128)}), f32[8,3,512]{2,1,0:T(4,128)S(1)}, u32[]{:S(2)}, u32[]{:S(2)}) async-start(f32[8,3,512]{2,1,0:T(4,128)} %broadcast_in_dim.2), calls=%async_computation | async-start | bytes 131072 | tf_op jit(solution)/shard_map/all_to_all | solution.py:40
  19.4 1.9 %collective-permute-start.1 = (bf16[2048,512]{1,0:T(8,128)(2,1)}, bf16[2048,512]{1,0:T(8,128)(2,1)}, u32[]{:S(2)}, u32[]{:S(2)}) collective-permute-start(bf16[2048,512]{1,0:T(8,128)(2,1)} %param.1), channel_id=1, source_target_pairs={{16,0},{18,2},{20,4},{22,6},{24,8},{26,10},{28,12},{30,14},{17,1},... | collective-permute-start | bytes 6291464 | tf_op jit(solution)/shard_map/ppermute | solution.py:36
  21.3 4.7 %collective-permute-start.4 = (bf16[2048,256]{1,0:T(8,128)(2,1)}, bf16[2048,256]{1,0:T(8,128)(2,1)}, u32[]{:S(2)}, u32[]{:S(2)}) collective-permute-start(bf16[2048,256]{1,0:T(8,128)(2,1)} %slice.39), channel_id=1, source_target_pairs={{32,0},{48,16},{34,2},{50,18},{36,4},{52,20},{38,6},{54,22},{40,8}... | collective-permute-start | bytes 3145736 | tf_op jit(solution)/shard_map/ppermute | solution.py:36
  26.0 1.8 all-to-all-done
  27.8 4.7 %collective-permute-start.5 = (f32[2,256]{1,0:T(2,128)S(1)}, f32[2,256]{1,0:T(2,128)S(1)}, u32[]{:S(2)}, u32[]{:S(2)}) collective-permute-start(f32[2,256]{1,0:T(2,128)S(1)} %fusion.51), channel_id=1, source_target_pairs={{32,0},{48,16},{34,2},{50,18},{36,4},{52,20},{38,6},{54,22},{40,8}... | collective-permute-start | bytes 6152 | tf_op jit(solution)/shard_map/ppermute | solution.py:36
  32.5 2.5 %fusion.7 = bf16[2048,512]{1,0:T(8,128)(2,1)S(1)} fusion(bf16[2048,512]{1,0:T(8,128)(2,1)} %param.1, f32[512]{0:T(512)S(1)} %bitcast.21, f32[512]{0:T(512)S(1)} %bitcast.22), kind=kLoop, calls=%fused_computation.11 | loop fusion | flops 7340032 | bytes 4198400 | tf_op jit(solution)/shard_map/convert_element_type | solution.py:46
  35.0 2.1 %fusion.40 = bf16[512,512]{1,0:T(8,128)(2,1)} fusion(bf16[2048,512]{1,0:T(8,128)(2,1)S(1)} %fusion.7), kind=kOutput, calls=%fused_computation.38 | convolution fusion | flops 1074266112 | bytes 2621440 | tf_op jit(solution)/shard_map/dot_general | solution.py:74
  37.1 1.0 slice.61
  38.1 2.5 %collective-permute-start.8 = (bf16[2048,256]{1,0:T(8,128)(2,1)}, bf16[2048,256]{1,0:T(8,128)(2,1)}, u32[]{:S(2)}, u32[]{:S(2)}) collective-permute-start(bf16[2048,256]{1,0:T(8,128)(2,1)} %slice.61), channel_id=1, source_target_pairs={{32,0},{48,16},{34,2},{50,18},{36,4},{52,20},{38,6},{54,22},{40,8}... | collective-permute-start | bytes 3145736 | tf_op jit(solution)/shard_map/ppermute | solution.py:36
  40.7 1.9 %collective-permute-start.2 = (f32[2,512]{1,0:T(2,128)S(1)}, f32[2,512]{1,0:T(2,128)S(1)}, u32[]{:S(2)}, u32[]{:S(2)}) collective-permute-start(f32[2,512]{1,0:T(2,128)S(1)} %pad_maximum_fusion.2), channel_id=1, source_target_pairs={{16,0},{18,2},{20,4},{22,6},{24,8},{26,10},{28,12},{30,14},{17,1},... | collective-permute-start | bytes 12296 | tf_op jit(solution)/shard_map/ppermute | solution.py:36
  42.6 5.5 %all-to-all-start.1 = ((bf16[8,64,512]{2,1,0:T(8,128)(2,1)}), bf16[8,64,512]{2,1,0:T(8,128)(2,1)S(1)}, u32[]{:S(2)}, u32[]{:S(2)}) async-start(bf16[8,64,512]{2,1,0:T(8,128)(2,1)} %bitcast.5), calls=%async_computation.1 | async-start | bytes 1048576 | tf_op jit(solution)/shard_map/all_to_all | solution.py:40
  48.1 30.8 %collective-permute-done.5 = f32[2,256]{1,0:T(2,128)S(1)} collective-permute-done((f32[2,256]{1,0:T(2,128)S(1)}, f32[2,256]{1,0:T(2,128)S(1)}, u32[]{:S(2)}, u32[]{:S(2)}) %collective-permute-start.5) | collective-permute-done | bytes 2080 | tf_op jit(solution)/shard_map/ppermute | solution.py:36
  78.9 11.3 %collective-permute-done.2 = f32[2,512]{1,0:T(2,128)S(1)} collective-permute-done((f32[2,512]{1,0:T(2,128)S(1)}, f32[2,512]{1,0:T(2,128)S(1)}, u32[]{:S(2)}, u32[]{:S(2)}) %collective-permute-start.2) | collective-permute-done | bytes 4128 | tf_op jit(solution)/shard_map/ppermute | solution.py:36
  90.1 0.0 collective-permute-done.4
  90.1 2.6 %fusion.14 = bf16[2048,256]{1,0:T(8,128)(2,1)} fusion(bf16[2048,256]{1,0:T(8,128)(2,1)} %collective-permute-done.4, f32[256]{0:T(256)S(1)} %bitcast.30, f32[256]{0:T(256)S(1)} %bitcast.29), kind=kLoop, calls=%fused_computation.20 | loop fusion | flops 3670016 | bytes 2099200 | tf_op jit(solution)/shard_map/convert_element_type | solution.py:46
  92.8 4.9 %collective-permute-start.6 = (bf16[2048,256]{1,0:T(8,128)(2,1)}, bf16[2048,256]{1,0:T(8,128)(2,1)}, u32[]{:S(2)}, u32[]{:S(2)}) collective-permute-start(bf16[2048,256]{1,0:T(8,128)(2,1)} %fusion.14), channel_id=1, source_target_pairs={{0,16},{16,0},{2,18},{18,2},{4,20},{20,4},{6,22},{22,6},{8,24},{24... | collective-permute-start | bytes 3145736 | tf_op jit(solution)/shard_map/ppermute | solution.py:36
  97.7 0.0 collective-permute-done.1
  97.7 3.8 %fusion.37 = bf16[512,512]{1,0:T(8,128)(2,1)} fusion(bf16[2048,512]{1,0:T(8,128)(2,1)S(1)} %fusion.7, bf16[2048,512]{1,0:T(8,128)(2,1)} %collective-permute-done.1, f32[512]{0:T(512)S(1)} %bitcast.32, f32[512]{0:T(512)S(1)} %bitcast.31), kind=kOutput, calls=%fused_computation.37 | convolution fusion | flops 1081606144 | bytes 4722688 | tf_op jit(solution)/shard_map/dot_general | solution.py:74
  101.4 0.0 all-to-all-done.1
  101.4 7.2 %all-to-all-start.2 = ((bf16[8,64,512]{2,1,0:T(8,128)(2,1)}), bf16[8,64,512]{2,1,0:T(8,128)(2,1)S(1)}, u32[]{:S(2)}, u32[]{:S(2)}) async-start(bf16[8,64,512]{2,1,0:T(8,128)(2,1)} %bitcast.19), calls=%async_computation.2 | async-start | bytes 1048576 | tf_op jit(solution)/shard_map/all_to_all | solution.py:40
  108.7 0.0 collective-permute-done.8
  108.7 1.9 %collective-permute-start.9 = (bf16[2048,256]{1,0:T(8,128)(2,1)}, bf16[2048,256]{1,0:T(8,128)(2,1)}, u32[]{:S(2)}, u32[]{:S(2)}) collective-permute-start(bf16[2048,256]{1,0:T(8,128)(2,1)} %collective-permute-done.8), channel_id=1, source_target_pairs={{0,16},{16,0},{2,18},{18,2},{4,20},{20,4},{6,22},{22,6},{8,24},{24... | collective-permute-start | bytes 3145736 | tf_op jit(solution)/shard_map/ppermute | solution.py:36
  110.6 0.0 collective-permute-done.6
  110.6 3.6 %fusion.41 = bf16[512,512]{1,0:T(8,128)(2,1)} fusion(bf16[2048,512]{1,0:T(8,128)(2,1)S(1)} %fusion.7, bf16[2048,256]{1,0:T(8,128)(2,1)} %collective-permute-done.6, bf16[2048,256]{1,0:T(8,128)(2,1)} %fusion.14), kind=kOutput, calls=%fused_computation.39 | convolution fusion | flops 1078460416 | bytes 4718592 | tf_op jit(solution)/shard_map/dot_general | solution.py:74
  114.2 12.1 %all-to-all-done.2 = bf16[8,64,512]{2,1,0:T(8,128)(2,1)S(1)} async-done(((bf16[8,64,512]{2,1,0:T(8,128)(2,1)}), bf16[8,64,512]{2,1,0:T(8,128)(2,1)S(1)}, u32[]{:S(2)}, u32[]{:S(2)}) %all-to-all-start.2) | async-done | bytes 524320 | tf_op jit(solution)/shard_map/all_to_all | solution.py:40
  126.3 4.1 %all-to-all-start.3 = ((bf16[8,64,512]{2,1,0:T(8,128)(2,1)}), bf16[8,64,512]{2,1,0:T(8,128)(2,1)}, u32[]{:S(2)}, u32[]{:S(2)}) async-start(bf16[8,64,512]{2,1,0:T(8,128)(2,1)} %bitcast.20), calls=%async_computation.3 | async-start | bytes 1048576 | tf_op jit(solution)/shard_map/all_to_all | solution.py:40
  130.5 0.0 collective-permute-done.9
  130.5 3.6 %fusion.44 = bf16[512,512]{1,0:T(8,128)(2,1)} fusion(bf16[2048,512]{1,0:T(8,128)(2,1)S(1)} %fusion.7, bf16[2048,256]{1,0:T(8,128)(2,1)} %collective-permute-done.9, bf16[2048,256]{1,0:T(8,128)(2,1)} %collective-permute-done.8), kind=kOutput, calls=%fused_computation.40 | convolution fusion | flops 1078460416 | bytes 4718592 | tf_op jit(solution)/shard_map/dot_general | solution.py:74
  134.1 14.3 %all-to-all-done.3 = bf16[8,64,512]{2,1,0:T(8,128)(2,1)} async-done(((bf16[8,64,512]{2,1,0:T(8,128)(2,1)}), bf16[8,64,512]{2,1,0:T(8,128)(2,1)}, u32[]{:S(2)}, u32[]{:S(2)}) %all-to-all-start.3) | async-done | bytes 524320 | tf_op jit(solution)/shard_map/all_to_all | solution.py:40
  148.4 3.5 %all-to-all-start.4 = ((bf16[8,64,512]{2,1,0:T(8,128)(2,1)}), bf16[8,64,512]{2,1,0:T(8,128)(2,1)S(1)}, u32[]{:S(2)}, u32[]{:S(2)}) async-start(bf16[8,64,512]{2,1,0:T(8,128)(2,1)} %bitcast.18), calls=%async_computation.4 | async-start | bytes 1048576 | tf_op jit(solution)/shard_map/all_to_all | solution.py:40
  152.0 0.1 convert_reduce_fusion.3
  152.0 0.1 convert_reduce_fusion.2
  152.1 1.1 convert_reduce_fusion.1
  153.3 3.3 %collective-permute-start.7 = (f32[32,512]{1,0:T(8,128)S(1)}, f32[32,512]{1,0:T(8,128)S(1)}, u32[]{:S(2)}, u32[]{:S(2)}) collective-permute-start(f32[32,512]{1,0:T(8,128)S(1)} %constant_dynamic-slice_fusion.1), channel_id=1, source_target_pairs={{0,1},{16,17},{2,3},{18,19},{4,5},{20,21},{6,7},{22,23},{8,9},{24,... | collective-permute-start | bytes 196616 | tf_op jit(solution)/shard_map/ppermute | solution.py:36
  156.6 2.6 %collective-permute-start.3 = (f32[32,1024]{1,0:T(8,128)S(1)}, f32[32,1024]{1,0:T(8,128)S(1)}, u32[]{:S(2)}, u32[]{:S(2)}) collective-permute-start(f32[32,1024]{1,0:T(8,128)S(1)} %fusion.47), channel_id=1, source_target_pairs={{0,1},{16,17},{2,3},{18,19},{4,5},{20,21},{6,7},{22,23},{8,9},{24,... | collective-permute-start | bytes 393224 | tf_op jit(solution)/shard_map/ppermute | solution.py:36
  159.1 0.3 collective-permute-done.7
  159.4 10.4 %all-to-all-done.4 = bf16[8,64,512]{2,1,0:T(8,128)(2,1)S(1)} async-done(((bf16[8,64,512]{2,1,0:T(8,128)(2,1)}), bf16[8,64,512]{2,1,0:T(8,128)(2,1)S(1)}, u32[]{:S(2)}, u32[]{:S(2)}) %all-to-all-start.4) | async-done | bytes 524320 | tf_op jit(solution)/shard_map/all_to_all | solution.py:40
  169.8 0.1 convert_reduce_fusion
  169.9 3.3 %collective-permute-start.10 = (f32[32,512]{1,0:T(8,128)S(1)}, f32[32,512]{1,0:T(8,128)S(1)}, u32[]{:S(2)}, u32[]{:S(2)}) collective-permute-start(f32[32,512]{1,0:T(8,128)S(1)} %constant_dynamic-slice_fusion), channel_id=1, source_target_pairs={{0,1},{16,17},{2,3},{18,19},{4,5},{20,21},{6,7},{22,23},{8,9},{24,... | collective-permute-start | bytes 196616 | tf_op jit(solution)/shard_map/ppermute | solution.py:36
  173.2 0.0 collective-permute-done.3
  173.2 2.8 %collective-permute-done.10 = f32[32,512]{1,0:T(8,128)S(1)} collective-permute-done((f32[32,512]{1,0:T(8,128)S(1)}, f32[32,512]{1,0:T(8,128)S(1)}, u32[]{:S(2)}, u32[]{:S(2)}) %collective-permute-start.10) | collective-permute-done | bytes 65568 | tf_op jit(solution)/shard_map/ppermute | solution.py:36
  176.1 0.0 copy-start
  176.1 0.7 copy-done
  176.8 0.6 select_dynamic-update-slice_fusion
  (20 shorter events, 0.2 us)
Async XLA Ops:
  2.7 5.7 %collective-permute-start = (f32[3,512]{1,0:T(4,128)S(1)}, f32[3,512]{1,0:T(4,128)S(1)}, u32[]{:S(2)}, u32[]{:S(2)}) collective-permute-start(f32[3,512]{1,0:T(4,128)S(1)} %pad_maximum_fusion.1), channel_id=1, source_target_pairs={{0,1},{16,17},{2,3},{18,19},{4,5},{20,21},{6,7},{22,23},{8,9},{24,... | collective-permute-start | bytes 18440 | tf_op jit(solution)/shard_map/ppermute | solution.py:36
  9.0 18.7 %all-to-all-start = ((f32[8,3,512]{2,1,0:T(4,128)}), f32[8,3,512]{2,1,0:T(4,128)S(1)}, u32[]{:S(2)}, u32[]{:S(2)}) async-start(f32[8,3,512]{2,1,0:T(4,128)} %broadcast_in_dim.2), calls=%async_computation | async-start | bytes 131072 | tf_op jit(solution)/shard_map/all_to_all | solution.py:40
  19.4 78.3 %collective-permute-start.1 = (bf16[2048,512]{1,0:T(8,128)(2,1)}, bf16[2048,512]{1,0:T(8,128)(2,1)}, u32[]{:S(2)}, u32[]{:S(2)}) collective-permute-start(bf16[2048,512]{1,0:T(8,128)(2,1)} %param.1), channel_id=1, source_target_pairs={{16,0},{18,2},{20,4},{22,6},{24,8},{26,10},{28,12},{30,14},{17,1},... | collective-permute-start | bytes 6291464 | tf_op jit(solution)/shard_map/ppermute | solution.py:36
  21.3 68.8 %collective-permute-start.4 = (bf16[2048,256]{1,0:T(8,128)(2,1)}, bf16[2048,256]{1,0:T(8,128)(2,1)}, u32[]{:S(2)}, u32[]{:S(2)}) collective-permute-start(bf16[2048,256]{1,0:T(8,128)(2,1)} %slice.39), channel_id=1, source_target_pairs={{32,0},{48,16},{34,2},{50,18},{36,4},{52,20},{38,6},{54,22},{40,8}... | collective-permute-start | bytes 3145736 | tf_op jit(solution)/shard_map/ppermute | solution.py:36
  27.8 51.0 %collective-permute-start.5 = (f32[2,256]{1,0:T(2,128)S(1)}, f32[2,256]{1,0:T(2,128)S(1)}, u32[]{:S(2)}, u32[]{:S(2)}) collective-permute-start(f32[2,256]{1,0:T(2,128)S(1)} %fusion.51), channel_id=1, source_target_pairs={{32,0},{48,16},{34,2},{50,18},{36,4},{52,20},{38,6},{54,22},{40,8}... | collective-permute-start | bytes 6152 | tf_op jit(solution)/shard_map/ppermute | solution.py:36
  38.1 70.5 %collective-permute-start.8 = (bf16[2048,256]{1,0:T(8,128)(2,1)}, bf16[2048,256]{1,0:T(8,128)(2,1)}, u32[]{:S(2)}, u32[]{:S(2)}) collective-permute-start(bf16[2048,256]{1,0:T(8,128)(2,1)} %slice.61), channel_id=1, source_target_pairs={{32,0},{48,16},{34,2},{50,18},{36,4},{52,20},{38,6},{54,22},{40,8}... | collective-permute-start | bytes 3145736 | tf_op jit(solution)/shard_map/ppermute | solution.py:36
  40.7 49.4 %collective-permute-start.2 = (f32[2,512]{1,0:T(2,128)S(1)}, f32[2,512]{1,0:T(2,128)S(1)}, u32[]{:S(2)}, u32[]{:S(2)}) collective-permute-start(f32[2,512]{1,0:T(2,128)S(1)} %pad_maximum_fusion.2), channel_id=1, source_target_pairs={{16,0},{18,2},{20,4},{22,6},{24,8},{26,10},{28,12},{30,14},{17,1},... | collective-permute-start | bytes 12296 | tf_op jit(solution)/shard_map/ppermute | solution.py:36
  42.6 58.8 %all-to-all-start.1 = ((bf16[8,64,512]{2,1,0:T(8,128)(2,1)}), bf16[8,64,512]{2,1,0:T(8,128)(2,1)S(1)}, u32[]{:S(2)}, u32[]{:S(2)}) async-start(bf16[8,64,512]{2,1,0:T(8,128)(2,1)} %bitcast.5), calls=%async_computation.1 | async-start | bytes 1048576 | tf_op jit(solution)/shard_map/all_to_all | solution.py:40
  92.8 17.8 %collective-permute-start.6 = (bf16[2048,256]{1,0:T(8,128)(2,1)}, bf16[2048,256]{1,0:T(8,128)(2,1)}, u32[]{:S(2)}, u32[]{:S(2)}) collective-permute-start(bf16[2048,256]{1,0:T(8,128)(2,1)} %fusion.14), channel_id=1, source_target_pairs={{0,16},{16,0},{2,18},{18,2},{4,20},{20,4},{6,22},{22,6},{8,24},{24... | collective-permute-start | bytes 3145736 | tf_op jit(solution)/shard_map/ppermute | solution.py:36
  101.4 24.9 %all-to-all-start.2 = ((bf16[8,64,512]{2,1,0:T(8,128)(2,1)}), bf16[8,64,512]{2,1,0:T(8,128)(2,1)S(1)}, u32[]{:S(2)}, u32[]{:S(2)}) async-start(bf16[8,64,512]{2,1,0:T(8,128)(2,1)} %bitcast.19), calls=%async_computation.2 | async-start | bytes 1048576 | tf_op jit(solution)/shard_map/all_to_all | solution.py:40
  108.7 21.8 %collective-permute-start.9 = (bf16[2048,256]{1,0:T(8,128)(2,1)}, bf16[2048,256]{1,0:T(8,128)(2,1)}, u32[]{:S(2)}, u32[]{:S(2)}) collective-permute-start(bf16[2048,256]{1,0:T(8,128)(2,1)} %collective-permute-done.8), channel_id=1, source_target_pairs={{0,16},{16,0},{2,18},{18,2},{4,20},{20,4},{6,22},{22,6},{8,24},{24... | collective-permute-start | bytes 3145736 | tf_op jit(solution)/shard_map/ppermute | solution.py:36
  126.3 22.1 %all-to-all-start.3 = ((bf16[8,64,512]{2,1,0:T(8,128)(2,1)}), bf16[8,64,512]{2,1,0:T(8,128)(2,1)}, u32[]{:S(2)}, u32[]{:S(2)}) async-start(bf16[8,64,512]{2,1,0:T(8,128)(2,1)} %bitcast.20), calls=%async_computation.3 | async-start | bytes 1048576 | tf_op jit(solution)/shard_map/all_to_all | solution.py:40
  148.4 21.4 %all-to-all-start.4 = ((bf16[8,64,512]{2,1,0:T(8,128)(2,1)}), bf16[8,64,512]{2,1,0:T(8,128)(2,1)S(1)}, u32[]{:S(2)}, u32[]{:S(2)}) async-start(bf16[8,64,512]{2,1,0:T(8,128)(2,1)} %bitcast.18), calls=%async_computation.4 | async-start | bytes 1048576 | tf_op jit(solution)/shard_map/all_to_all | solution.py:40
  153.3 6.2 %collective-permute-start.7 = (f32[32,512]{1,0:T(8,128)S(1)}, f32[32,512]{1,0:T(8,128)S(1)}, u32[]{:S(2)}, u32[]{:S(2)}) collective-permute-start(f32[32,512]{1,0:T(8,128)S(1)} %constant_dynamic-slice_fusion.1), channel_id=1, source_target_pairs={{0,1},{16,17},{2,3},{18,19},{4,5},{20,21},{6,7},{22,23},{8,9},{24,... | collective-permute-start | bytes 196616 | tf_op jit(solution)/shard_map/ppermute | solution.py:36
  156.6 16.6 %collective-permute-start.3 = (f32[32,1024]{1,0:T(8,128)S(1)}, f32[32,1024]{1,0:T(8,128)S(1)}, u32[]{:S(2)}, u32[]{:S(2)}) collective-permute-start(f32[32,1024]{1,0:T(8,128)S(1)} %fusion.47), channel_id=1, source_target_pairs={{0,1},{16,17},{2,3},{18,19},{4,5},{20,21},{6,7},{22,23},{8,9},{24,... | collective-permute-start | bytes 393224 | tf_op jit(solution)/shard_map/ppermute | solution.py:36
  169.9 6.2 %collective-permute-start.10 = (f32[32,512]{1,0:T(8,128)S(1)}, f32[32,512]{1,0:T(8,128)S(1)}, u32[]{:S(2)}, u32[]{:S(2)}) collective-permute-start(f32[32,512]{1,0:T(8,128)S(1)} %constant_dynamic-slice_fusion), channel_id=1, source_target_pairs={{0,1},{16,17},{2,3},{18,19},{4,5},{20,21},{6,7},{22,23},{8,9},{24,... | collective-permute-start | bytes 196616 | tf_op jit(solution)/shard_map/ppermute | solution.py:36
  176.1 0.7 copy-start

commit v2 on v1

v2 whole, which is shorter than its diff:
```python
import jax
import jax.numpy as jnp
from jax import lax
from jax.sharding import PartitionSpec as P


TILE = 512
AXES = ("band", "samp")
YS, XS, ZS, CORES = 8, 4, 8, 2


def index_of(y, x, z, core):
    return ((y * 2 + x // 2) * CORES + core) * (ZS * 2) + z * 2 + x % 2


def pairs_of(target_of):
    pairs = []
    for y in range(YS):
        for x in range(XS):
            for z in range(ZS):
                for core in range(CORES):
                    target = target_of(y, x, z, core)
                    if target is not None and target[0] >= 0:
                        pairs.append((index_of(y, x, z, core), index_of(*target)))
    return pairs


NEXT_CHIP = pairs_of(lambda y, x, z, c: (y, x - 2, z, c) if x >= 2 else (y - 1, x + 2, z, c))
EDGE = pairs_of(lambda y, x, z, c: (y, x, z, 0) if c == 1 else (y - 1, x, z, 1))
OTHER_CORE = pairs_of(lambda y, x, z, c: (y, x, z, 1 - c))
OTHER_HALF = pairs_of(lambda y, x, z, c: (y, x ^ 1, z, c))
Z_GROUPS = [[low + 2 * z for z in range(ZS)] for low in range(2)]


def sent(value, pairs):
    return lax.ppermute(value, AXES, pairs)


def over_z(value):
    return lax.all_to_all(value, "samp", 0, 0, tiled=True, axis_index_groups=Z_GROUPS)


def over_samp(value):
    return lax.all_to_all(value, "samp", 0, 0, tiled=True)


def standardized(raw, stats):
    raw = raw.astype(jnp.float32)
    observed = (raw >= 0.0).astype(jnp.float32)
    return (observed * (observed * raw - stats[0]) * stats[1]).astype(jnp.bfloat16)


def assemble(even, own, edge, first_next, first_swap, last):
    half = first_next.shape[1]
    last = last.astype(jnp.float32).sum(0)
    nexts = jnp.concatenate([first_next, last[:, :half]], axis=1)
    swaps = jnp.concatenate([first_swap, last[:, half:]], axis=1)
    return jnp.concatenate(
        [own, jnp.where(even, edge, swaps), nexts, jnp.where(even, swaps, edge)], axis=1
    )


def on_device(dosage):
    half = TILE // 2
    samples = dosage.shape[0] * lax.axis_size("samp")
    even = lax.axis_index("band") % 2 == 0
    low = lax.axis_index("samp") % 2

    edge_raw = sent(dosage, EDGE)
    raw = dosage.astype(jnp.float32)
    observed = (raw >= 0.0).astype(jnp.float32)
    values = observed * raw
    sums = jnp.stack([observed.sum(0), values.sum(0), (values * values).sum(0)])
    everyone = over_samp(jnp.broadcast_to(sums[None], (2 * ZS, *sums.shape)))
    count, total, square = everyone.sum(0)
    mean = (total + 1.0) / (count + 1.0)
    spread = (square - 2.0 * mean * total + count * mean * mean + 0.5) / (count + 1.0)
    stats = jnp.stack([mean, lax.rsqrt(spread)])
    scaled = standardized(dosage, stats)
    next_a = sent(scaled[:, :half], NEXT_CHIP)
    edge_stats = sent(stats, EDGE)
    next_b = sent(scaled[:, half:], NEXT_CHIP)

    def tile(panel):
        product = lax.dot_general(
            scaled, panel, (((0,), (0,)), ((), ())), preferred_element_type=jnp.float32
        )
        return (product / samples).astype(jnp.bfloat16)

    own = tile(scaled)
    edge = tile(standardized(edge_raw, edge_stats))
    early = jnp.concatenate([own, edge], axis=1)
    early = over_z(early.reshape(ZS, -1, 2 * TILE)).astype(jnp.float32).sum(0)
    swap_a = sent(next_a, OTHER_CORE)
    mid = tile(jnp.concatenate([next_a, swap_a], axis=1))
    mid = over_samp(mid.reshape(2 * ZS, -1, TILE)).astype(jnp.float32).sum(0)
    count = early.shape[0] // 2
    mine = lax.dynamic_slice_in_dim(early, low * count, count, 0)
    other = lax.dynamic_slice_in_dim(early, (1 - low) * count, count, 0)
    early = mine + sent(other, OTHER_HALF)
    swap_b = sent(next_b, OTHER_CORE)
    last = tile(jnp.concatenate([next_b, swap_b], axis=1))
    last = over_samp(last.reshape(2 * ZS, -1, TILE))
    return assemble(even, early[:, :TILE], early[:, TILE:], mid[:, :half], mid[:, half:], last)


def solution(mesh):
    return jax.shard_map(
        on_device,
        mesh=mesh,
        in_specs=(P("samp", "band"),),
        out_specs=P(("band", "samp"), None),
        check_vma=False,
    )
```

time: 179 us -> 140 us (0.78)
  starting transfers between devices: 65.7 us -> 34.9 us
  waiting for transfers between devices: 83.7 us -> 59.5 us
  blocking collectives: 0 us -> 20.8 us
  other arithmetic: 9.97 us -> 5.94 us
  matrix products: 13.1 us -> 11.2 us
    all_to_all x5 -> x1, waiting for transfers between devices: 38.6 us -> 1.64 us  [over_z(): lax.all_to_all(value, 'samp', 0, 0, tiled=True, axis_index_groups=Z_GROUPS)]
    all_to_all x5 -> x1, starting transfers between devices: 30.6 us -> 3.56 us  [over_z(): lax.all_to_all(value, 'samp', 0, 0, tiled=True, axis_index_groups=Z_GROUPS)]
    all_to_all x0 -> x1, blocking collectives: none -> 20.8 us  [over_samp(): return lax.all_to_all(value, 'samp', 0, 0, tiled=True)]
    all_to_all x0 -> x2, waiting for transfers between devices: none -> 17.2 us  [over_samp(): return lax.all_to_all(value, 'samp', 0, 0, tiled=True)]
    ppermute x11 -> x7, starting transfers between devices: 35.1 us -> 21.9 us  [sent(): return lax.ppermute(value, AXES, pairs)]
    all_to_all x0 -> x2, starting transfers between devices: none -> 9.45 us  [over_samp(): return lax.all_to_all(value, 'samp', 0, 0, tiled=True)]
    ppermute x11 -> x7, waiting for transfers between devices: 45.2 us -> 40.7 us  [sent(): return lax.ppermute(value, AXES, pairs)]
    convert_element_type x2 -> x1, other arithmetic: 5.15 us -> 0.91 us  [standardized(): (observed * (observed * raw - stats[0]) * stats[1]).astype(jnp.bfloat16)]
  transfers between devices with their start and end apart: 16 -> 10, of which waited for: 8 -> 8; matrix products, arithmetic and copies ran while one was open for 13% -> 12% of each run, Pallas kernels for 0% -> 0%
where the time goes in v2:
time: 140 us; the launch traced here: 139 us
  waiting for transfers between devices  59.5 us (42%)
  starting transfers between devices  34.9 us (25%)
  blocking collectives  20.8 us (15%)
  matrix products  11.2 us (8%)
  local copies, waits for them, and re-layouts  6.36 us (5%)
  other arithmetic  5.94 us (4%)
    ppermute x7, waiting for transfers between devices, sent(): return lax.ppermute(value, AXES, pairs)  40.7 us
    ppermute x7, starting transfers between devices, sent(): return lax.ppermute(value, AXES, pairs)  21.9 us
    all_to_all x1, blocking collectives, over_samp(): return lax.all_to_all(value, 'samp', 0, 0, tiled=True)  20.8 us
    all_to_all x2, waiting for transfers between devices, over_samp(): return lax.all_to_all(value, 'samp', 0, 0, tiled=True)  17.2 us
    dot_general x4, matrix products, tile(): lax.dot_general(scaled, panel, (((0,), (0,)), ((), ())), preferred_elemen...  11.2 us
    all_to_all x2, starting transfers between devices, over_samp(): return lax.all_to_all(value, 'samp', 0, 0, tiled=True)  9.45 us
    all_to_all x1, starting transfers between devices, over_z(): lax.all_to_all(value, 'samp', 0, 0, tiled=True, axis_index_groups=Z_GROUPS)  3.56 us
    convert_element_type x2, local copies, waits for them, and re-layouts, tile(): return (product / samples).astype(jnp.bfloat16)  3.05 us
  transfers between devices with their start and end apart: 10, of which 8 were waited for; matrix products, arithmetic and copies ran while one was open for 12% of the time, Pallas kernels for 0%

profile of v2, /device:TPU:24, one launch (start us, length us, event | category | flops | bytes accessed | tf_op | source)
XLA Modules:
  0.0 139.0 jit_solution(4285128838737172217)
XLA Ops:
  0.0 0.0 copy-start
  0.0 2.8 %fusion.5 = (f32[512]{0:T(512)S(1)}, f32[512]{0:T(512)S(1)}, f32[512]{0:T(512)S(1)}) fusion(bf16[2048,512]{1,0:T(8,128)(2,1)} %param.1), kind=kLoop, calls=%fused_computation.9 | loop fusion | flops 8387072 | bytes 2103296 | tf_op jit(solution)/shard_map/reduce_sum | solution.py:73
  2.9 20.8 %all_to_all.20 = f32[16,3,512]{2,1,0:T(4,128)S(1)} all-to-all(f32[16,3,512]{2,1,0:T(4,128)S(1)} %broadcast_in_dim.2), channel_id=1, replica_groups=mesh['band'=32,'samp'=16] {'samp'}, dimensions={0} | all-to-all | bytes 196608 | tf_op jit(solution)/shard_map/all_to_all | solution.py:44
  23.7 0.0 copy-done
  23.7 0.9 fusion.7
  24.6 0.0 copy-start.1
  24.7 1.2 fusion.49
  25.9 4.5 %collective-permute-start.3 = (bf16[2048,256]{1,0:T(8,128)(2,1)S(1)}, bf16[2048,256]{1,0:T(8,128)(2,1)S(1)}, u32[]{:S(2)}, u32[]{:S(2)}) collective-permute-start(bf16[2048,256]{1,0:T(8,128)(2,1)S(1)} %get-tuple-element.10), channel_id=1, source_target_pairs={{32,0},{48,16},{34,2},{50,18},{36,4},{52,20},{38,6},{54,22},{40,8}... | collective-permute-start | bytes 3145736 | tf_op jit(solution)/shard_map/ppermute | solution.py:36
  30.4 1.9 %collective-permute-start = (bf16[2048,512]{1,0:T(8,128)(2,1)S(1)}, bf16[2048,512]{1,0:T(8,128)(2,1)}, u32[]{:S(2)}, u32[]{:S(2)}) collective-permute-start(bf16[2048,512]{1,0:T(8,128)(2,1)S(1)} %copy-done), channel_id=1, source_target_pairs={{16,0},{18,2},{20,4},{22,6},{24,8},{26,10},{28,12},{30,14},{17,1},... | collective-permute-start | bytes 6291464 | tf_op jit(solution)/shard_map/ppermute | solution.py:36
  32.3 20.4 %collective-permute-done.3 = bf16[2048,256]{1,0:T(8,128)(2,1)S(1)} collective-permute-done((bf16[2048,256]{1,0:T(8,128)(2,1)S(1)}, bf16[2048,256]{1,0:T(8,128)(2,1)S(1)}, u32[]{:S(2)}, u32[]{:S(2)}) %collective-permute-start.3) | collective-permute-done | bytes 1048608 | tf_op jit(solution)/shard_map/ppermute | solution.py:36
  52.7 1.9 %collective-permute-start.4 = (bf16[2048,256]{1,0:T(8,128)(2,1)S(1)}, bf16[2048,256]{1,0:T(8,128)(2,1)S(1)}, u32[]{:S(2)}, u32[]{:S(2)}) collective-permute-start(bf16[2048,256]{1,0:T(8,128)(2,1)S(1)} %collective-permute-done.3), channel_id=1, source_target_pairs={{0,16},{16,0},{2,18},{18,2},{4,20},{20,4},{6,22},{22,6},{8,24},{24... | collective-permute-start | bytes 3145736 | tf_op jit(solution)/shard_map/ppermute | solution.py:36
  54.6 2.5 %collective-permute-start.1 = (f32[2,512]{1,0:T(2,128)S(1)}, f32[2,512]{1,0:T(2,128)S(1)}, u32[]{:S(2)}, u32[]{:S(2)}) collective-permute-start(f32[2,512]{1,0:T(2,128)S(1)} %pad_maximum_fusion.3), channel_id=1, source_target_pairs={{16,0},{18,2},{20,4},{22,6},{24,8},{26,10},{28,12},{30,14},{17,1},... | collective-permute-start | bytes 12296 | tf_op jit(solution)/shard_map/ppermute | solution.py:36
  57.1 0.1 collective-permute-done.4
  57.3 0.0 copy-done.1
  57.3 1.3 fusion.38
  58.6 1.0 copy.17
  59.6 4.2 %all-to-all-start.2 = ((bf16[16,32,512]{2,1,0:T(8,128)(2,1)}), bf16[16,32,512]{2,1,0:T(8,128)(2,1)}, u32[]{:S(2)}, u32[]{:S(2)}) async-start(bf16[16,32,512]{2,1,0:T(8,128)(2,1)} %bitcast.8), calls=%async_computation.2 | async-start | bytes 1048576 | tf_op jit(solution)/shard_map/all_to_all | solution.py:44
  63.8 0.0 copy-start.2
  63.8 3.7 %fusion.37 = bf16[512,512]{0,1:T(8,128)(2,1)S(1)} fusion(bf16[2048,512]{1,0:T(8,128)(2,1)} %copy-done.1), kind=kOutput, calls=%fused_computation.34 | convolution fusion | flops 1074266112 | bytes 2621440 | tf_op jit(solution)/shard_map/dot_general | solution.py:85
  67.5 5.4 %collective-permute-start.5 = (bf16[2048,256]{1,0:T(8,128)(2,1)}, bf16[2048,256]{1,0:T(8,128)(2,1)}, u32[]{:S(2)}, u32[]{:S(2)}) collective-permute-start(bf16[2048,256]{1,0:T(8,128)(2,1)} %get-tuple-element.11), channel_id=1, source_target_pairs={{32,0},{48,16},{34,2},{50,18},{36,4},{52,20},{38,6},{54,22},{40,8}... | collective-permute-start | bytes 3145736 | tf_op jit(solution)/shard_map/ppermute | solution.py:36
  72.9 1.4 %collective-permute-done.1 = f32[2,512]{1,0:T(2,128)S(1)} collective-permute-done((f32[2,512]{1,0:T(2,128)S(1)}, f32[2,512]{1,0:T(2,128)S(1)}, u32[]{:S(2)}, u32[]{:S(2)}) %collective-permute-start.1) | collective-permute-done | bytes 4128 | tf_op jit(solution)/shard_map/ppermute | solution.py:36
  74.3 0.0 collective-permute-done
  74.4 0.0 copy-done.2
  74.4 2.9 %fusion.34 = bf16[512,512]{0,1:T(8,128)(2,1)S(1)} fusion(bf16[2048,512]{1,0:T(8,128)(2,1)S(1)} %copy-done.2, bf16[2048,512]{1,0:T(8,128)(2,1)} %collective-permute-done, f32[512]{0:T(512)S(1)} %bitcast.22, f32[512]{0:T(512)S(1)} %bitcast.21), kind=kOutput, calls=%fused_computation.33 | convolution fusion | flops 1081606144 | bytes 4722688 | tf_op jit(solution)/shard_map/dot_general | solution.py:85
  77.3 0.1 pad_maximum_fusion
  77.4 0.0 copy-start.3
  77.4 1.3 copy.15
  78.7 4.4 %all-to-all-done.2 = bf16[16,32,512]{2,1,0:T(8,128)(2,1)} async-done(((bf16[16,32,512]{2,1,0:T(8,128)(2,1)}), bf16[16,32,512]{2,1,0:T(8,128)(2,1)}, u32[]{:S(2)}, u32[]{:S(2)}) %all-to-all-start.2) | async-done | bytes 524320 | tf_op jit(solution)/shard_map/all_to_all | solution.py:44
  83.1 3.6 %all-to-all-start.1 = ((bf16[8,64,1024]{2,1,0:T(8,128)(2,1)}), bf16[8,64,1024]{2,1,0:T(8,128)(2,1)S(1)}, u32[]{:S(2)}, u32[]{:S(2)}) async-start(bf16[8,64,1024]{2,1,0:T(8,128)(2,1)} %bitcast.15), calls=%async_computation.1 | async-start | bytes 2097152 | tf_op jit(solution)/shard_map/all_to_all | solution.py:40
  86.7 15.9 %collective-permute-done.5 = bf16[2048,256]{1,0:T(8,128)(2,1)} collective-permute-done((bf16[2048,256]{1,0:T(8,128)(2,1)}, bf16[2048,256]{1,0:T(8,128)(2,1)}, u32[]{:S(2)}, u32[]{:S(2)}) %collective-permute-start.5) | collective-permute-done | bytes 1048608 | tf_op jit(solution)/shard_map/ppermute | solution.py:36
  102.6 1.9 %collective-permute-start.6 = (bf16[2048,256]{1,0:T(8,128)(2,1)}, bf16[2048,256]{1,0:T(8,128)(2,1)S(1)}, u32[]{:S(2)}, u32[]{:S(2)}) collective-permute-start(bf16[2048,256]{1,0:T(8,128)(2,1)} %collective-permute-done.5), channel_id=1, source_target_pairs={{0,16},{16,0},{2,18},{18,2},{4,20},{20,4},{6,22},{22,6},{8,24},{24... | collective-permute-start | bytes 3145736 | tf_op jit(solution)/shard_map/ppermute | solution.py:36
  104.5 2.8 %collective-permute-done.6 = bf16[2048,256]{1,0:T(8,128)(2,1)S(1)} collective-permute-done((bf16[2048,256]{1,0:T(8,128)(2,1)}, bf16[2048,256]{1,0:T(8,128)(2,1)S(1)}, u32[]{:S(2)}, u32[]{:S(2)}) %collective-permute-start.6) | collective-permute-done | bytes 1048608 | tf_op jit(solution)/shard_map/ppermute | solution.py:36
  107.3 0.0 copy-done.3
  107.3 3.3 %fusion.41 = bf16[512,512]{0,1:T(8,128)(2,1)} fusion(bf16[2048,512]{1,0:T(8,128)(2,1)S(1)} %copy-done.3, bf16[2048,256]{1,0:T(8,128)(2,1)S(1)} %collective-permute-done.6, bf16[2048,256]{1,0:T(8,128)(2,1)} %collective-permute-done.5), kind=kOutput, calls=%fused_computation.36 | convolution fusion | flops 1078460416 | bytes 4718592 | tf_op jit(solution)/shard_map/dot_general | solution.py:85
  110.7 2.0 %copy.19 = bf16[512,512]{1,0:T(8,128)(2,1)} copy(bf16[512,512]{0,1:T(8,128)(2,1)} %fusion.41) | data formatting | bytes 1048576 | tf_op jit(solution)/shard_map/convert_element_type | solution.py:88
  112.7 1.6 %all-to-all-done.1 = bf16[8,64,1024]{2,1,0:T(8,128)(2,1)S(1)} async-done(((bf16[8,64,1024]{2,1,0:T(8,128)(2,1)}), bf16[8,64,1024]{2,1,0:T(8,128)(2,1)S(1)}, u32[]{:S(2)}, u32[]{:S(2)}) %all-to-all-start.1) | async-done | bytes 1048608 | tf_op jit(solution)/shard_map/all_to_all | solution.py:40
  114.3 5.2 %all-to-all-start.3 = ((bf16[16,32,512]{2,1,0:T(8,128)(2,1)}), bf16[16,32,512]{2,1,0:T(8,128)(2,1)S(1)}, u32[]{:S(2)}, u32[]{:S(2)}) async-start(bf16[16,32,512]{2,1,0:T(8,128)(2,1)} %bitcast.9), calls=%async_computation.3 | async-start | bytes 1048576 | tf_op jit(solution)/shard_map/all_to_all | solution.py:44
  119.6 1.1 convert_reduce_fusion.2
  120.7 0.2 convert_reduce_fusion
  120.9 3.8 %collective-permute-start.2 = (f32[32,1024]{1,0:T(8,128)S(1)}, f32[32,1024]{1,0:T(8,128)S(1)}, u32[]{:S(2)}, u32[]{:S(2)}) collective-permute-start(f32[32,1024]{1,0:T(8,128)S(1)} %constant_dynamic-slice_fusion), channel_id=1, source_target_pairs={{0,1},{16,17},{2,3},{18,19},{4,5},{20,21},{6,7},{22,23},{8,9},{24,... | collective-permute-start | bytes 393224 | tf_op jit(solution)/shard_map/ppermute | solution.py:36
  124.7 12.8 %all-to-all-done.3 = bf16[16,32,512]{2,1,0:T(8,128)(2,1)S(1)} async-done(((bf16[16,32,512]{2,1,0:T(8,128)(2,1)}), bf16[16,32,512]{2,1,0:T(8,128)(2,1)S(1)}, u32[]{:S(2)}, u32[]{:S(2)}) %all-to-all-start.3) | async-done | bytes 524320 | tf_op jit(solution)/shard_map/all_to_all | solution.py:44
  137.5 0.1 convert_reduce_fusion.1
  137.6 0.0 collective-permute-done.2
  137.7 0.0 copy-start.4
  137.7 0.7 copy-done.4
  138.4 0.6 select_dynamic-update-slice_fusion
  (14 shorter events, 0.2 us)
Async XLA Ops:
  0.0 23.7 %copy-start = (bf16[2048,512]{1,0:T(8,128)(2,1)S(1)}, bf16[2048,512]{1,0:T(8,128)(2,1)}, u32[]{:S(2)}) copy-start(bf16[2048,512]{1,0:T(8,128)(2,1)} %param.1) | copy-start | bytes 6291460
  24.6 32.6 %copy-start.1 = (bf16[2048,512]{1,0:T(8,128)(2,1)}, bf16[2048,512]{1,0:T(8,128)(2,1)S(1)}, u32[]{:S(2)}) copy-start(bf16[2048,512]{1,0:T(8,128)(2,1)S(1)} %fusion.7) | copy-start | bytes 6291460
  25.9 26.9 %collective-permute-start.3 = (bf16[2048,256]{1,0:T(8,128)(2,1)S(1)}, bf16[2048,256]{1,0:T(8,128)(2,1)S(1)}, u32[]{:S(2)}, u32[]{:S(2)}) collective-permute-start(bf16[2048,256]{1,0:T(8,128)(2,1)S(1)} %get-tuple-element.10), channel_id=1, source_target_pairs={{32,0},{48,16},{34,2},{50,18},{36,4},{52,20},{38,6},{54,22},{40,8}... | collective-permute-start | bytes 3145736 | tf_op jit(solution)/shard_map/ppermute | solution.py:36
  30.4 44.0 %collective-permute-start = (bf16[2048,512]{1,0:T(8,128)(2,1)S(1)}, bf16[2048,512]{1,0:T(8,128)(2,1)}, u32[]{:S(2)}, u32[]{:S(2)}) collective-permute-start(bf16[2048,512]{1,0:T(8,128)(2,1)S(1)} %copy-done), channel_id=1, source_target_pairs={{16,0},{18,2},{20,4},{22,6},{24,8},{26,10},{28,12},{30,14},{17,1},... | collective-permute-start | bytes 6291464 | tf_op jit(solution)/shard_map/ppermute | solution.py:36
  52.7 4.5 %collective-permute-start.4 = (bf16[2048,256]{1,0:T(8,128)(2,1)S(1)}, bf16[2048,256]{1,0:T(8,128)(2,1)S(1)}, u32[]{:S(2)}, u32[]{:S(2)}) collective-permute-start(bf16[2048,256]{1,0:T(8,128)(2,1)S(1)} %collective-permute-done.3), channel_id=1, source_target_pairs={{0,16},{16,0},{2,18},{18,2},{4,20},{20,4},{6,22},{22,6},{8,24},{24... | collective-permute-start | bytes 3145736 | tf_op jit(solution)/shard_map/ppermute | solution.py:36
  54.6 19.7 %collective-permute-start.1 = (f32[2,512]{1,0:T(2,128)S(1)}, f32[2,512]{1,0:T(2,128)S(1)}, u32[]{:S(2)}, u32[]{:S(2)}) collective-permute-start(f32[2,512]{1,0:T(2,128)S(1)} %pad_maximum_fusion.3), channel_id=1, source_target_pairs={{16,0},{18,2},{20,4},{22,6},{24,8},{26,10},{28,12},{30,14},{17,1},... | collective-permute-start | bytes 12296 | tf_op jit(solution)/shard_map/ppermute | solution.py:36
  59.6 23.5 %all-to-all-start.2 = ((bf16[16,32,512]{2,1,0:T(8,128)(2,1)}), bf16[16,32,512]{2,1,0:T(8,128)(2,1)}, u32[]{:S(2)}, u32[]{:S(2)}) async-start(bf16[16,32,512]{2,1,0:T(8,128)(2,1)} %bitcast.8), calls=%async_computation.2 | async-start | bytes 1048576 | tf_op jit(solution)/shard_map/all_to_all | solution.py:44
  63.8 10.5 %copy-start.2 = (bf16[2048,512]{1,0:T(8,128)(2,1)S(1)}, bf16[2048,512]{1,0:T(8,128)(2,1)}, u32[]{:S(2)}) copy-start(bf16[2048,512]{1,0:T(8,128)(2,1)} %copy-done.1) | copy-start | bytes 6291460
  67.5 35.1 %collective-permute-start.5 = (bf16[2048,256]{1,0:T(8,128)(2,1)}, bf16[2048,256]{1,0:T(8,128)(2,1)}, u32[]{:S(2)}, u32[]{:S(2)}) collective-permute-start(bf16[2048,256]{1,0:T(8,128)(2,1)} %get-tuple-element.11), channel_id=1, source_target_pairs={{32,0},{48,16},{34,2},{50,18},{36,4},{52,20},{38,6},{54,22},{40,8}... | collective-permute-start | bytes 3145736 | tf_op jit(solution)/shard_map/ppermute | solution.py:36
  77.4 30.0 %copy-start.3 = (bf16[2048,512]{1,0:T(8,128)(2,1)S(1)}, bf16[2048,512]{1,0:T(8,128)(2,1)}, u32[]{:S(2)}) copy-start(bf16[2048,512]{1,0:T(8,128)(2,1)} %copy-done.1) | copy-start | bytes 6291460
  83.1 31.2 %all-to-all-start.1 = ((bf16[8,64,1024]{2,1,0:T(8,128)(2,1)}), bf16[8,64,1024]{2,1,0:T(8,128)(2,1)S(1)}, u32[]{:S(2)}, u32[]{:S(2)}) async-start(bf16[8,64,1024]{2,1,0:T(8,128)(2,1)} %bitcast.15), calls=%async_computation.1 | async-start | bytes 2097152 | tf_op jit(solution)/shard_map/all_to_all | solution.py:40
  102.6 4.8 %collective-permute-start.6 = (bf16[2048,256]{1,0:T(8,128)(2,1)}, bf16[2048,256]{1,0:T(8,128)(2,1)S(1)}, u32[]{:S(2)}, u32[]{:S(2)}) collective-permute-start(bf16[2048,256]{1,0:T(8,128)(2,1)} %collective-permute-done.5), channel_id=1, source_target_pairs={{0,16},{16,0},{2,18},{18,2},{4,20},{20,4},{6,22},{22,6},{8,24},{24... | collective-permute-start | bytes 3145736 | tf_op jit(solution)/shard_map/ppermute | solution.py:36
  114.3 23.2 %all-to-all-start.3 = ((bf16[16,32,512]{2,1,0:T(8,128)(2,1)}), bf16[16,32,512]{2,1,0:T(8,128)(2,1)S(1)}, u32[]{:S(2)}, u32[]{:S(2)}) async-start(bf16[16,32,512]{2,1,0:T(8,128)(2,1)} %bitcast.9), calls=%async_computation.3 | async-start | bytes 1048576 | tf_op jit(solution)/shard_map/all_to_all | solution.py:44
  120.9 16.7 %collective-permute-start.2 = (f32[32,1024]{1,0:T(8,128)S(1)}, f32[32,1024]{1,0:T(8,128)S(1)}, u32[]{:S(2)}, u32[]{:S(2)}) collective-permute-start(f32[32,1024]{1,0:T(8,128)S(1)} %constant_dynamic-slice_fusion), channel_id=1, source_target_pairs={{0,1},{16,17},{2,3},{18,19},{4,5},{20,21},{6,7},{22,23},{8,9},{24,... | collective-permute-start | bytes 393224 | tf_op jit(solution)/shard_map/ppermute | solution.py:36
  137.7 0.7 copy-start.4

commit v3 on v2

--- a/solution.py
+++ b/solution.py
@@ -1,6 +1,7 @@
 import jax
 import jax.numpy as jnp
 from jax import lax
+from jax.experimental.layout import Layout, with_layout_constraint
 from jax.sharding import PartitionSpec as P
 
 
@@ -50,13 +51,22 @@
     return (observed * (observed * raw - stats[0]) * stats[1]).astype(jnp.bfloat16)
 
 
-def assemble(even, own, edge, first_next, first_swap, last):
-    half = first_next.shape[1]
-    last = last.astype(jnp.float32).sum(0)
-    nexts = jnp.concatenate([first_next, last[:, :half]], axis=1)
-    swaps = jnp.concatenate([first_swap, last[:, half:]], axis=1)
+def assembled(even, early, mid, last):
+    half = mid.shape[1] // 2
+    own, edge = early[:, :TILE], early[:, TILE:]
+    low, high, next_low, next_high = mid[:, half:], last[:, half:], mid[:, :half], last[:, :half]
+    edge_low, edge_high = edge[:, :half], edge[:, half:]
     return jnp.concatenate(
-        [own, jnp.where(even, edge, swaps), nexts, jnp.where(even, swaps, edge)], axis=1
+        [
+            own,
+            jnp.where(even, edge_low, low),
+            jnp.where(even, edge_high, high),
+            next_low,
+            next_high,
+            jnp.where(even, low, edge_low),
+            jnp.where(even, high, edge_high),
+        ],
+        axis=1,
     )
 
 
@@ -76,16 +86,18 @@
     mean = (total + 1.0) / (count + 1.0)
     spread = (square - 2.0 * mean * total + count * mean * mean + 0.5) / (count + 1.0)
     stats = jnp.stack([mean, lax.rsqrt(spread)])
+    edge_stats = sent(stats, EDGE)
+    next_a = sent(standardized(dosage[:, :half], stats[:, :half]), NEXT_CHIP)
     scaled = standardized(dosage, stats)
-    next_a = sent(scaled[:, :half], NEXT_CHIP)
-    edge_stats = sent(stats, EDGE)
+    scaled = lax.optimization_barrier(scaled)
     next_b = sent(scaled[:, half:], NEXT_CHIP)
 
     def tile(panel):
         product = lax.dot_general(
             scaled, panel, (((0,), (0,)), ((), ())), preferred_element_type=jnp.float32
         )
-        return (product / samples).astype(jnp.bfloat16)
+        product = (product / samples).astype(jnp.bfloat16)
+        return with_layout_constraint(product, Layout(major_to_minor=(0, 1)))
 
     own = tile(scaled)
     edge = tile(standardized(edge_raw, edge_stats))
@@ -93,15 +105,20 @@
     early = over_z(early.reshape(ZS, -1, 2 * TILE)).astype(jnp.float32).sum(0)
     swap_a = sent(next_a, OTHER_CORE)
     mid = tile(jnp.concatenate([next_a, swap_a], axis=1))
-    mid = over_samp(mid.reshape(2 * ZS, -1, TILE)).astype(jnp.float32).sum(0)
+    mid = over_z(mid.reshape(ZS, -1, TILE)).astype(jnp.float32).sum(0)
     count = early.shape[0] // 2
-    mine = lax.dynamic_slice_in_dim(early, low * count, count, 0)
-    other = lax.dynamic_slice_in_dim(early, (1 - low) * count, count, 0)
-    early = mine + sent(other, OTHER_HALF)
+
+    def pair_sum(rows):
+        mine = lax.dynamic_slice_in_dim(rows, low * count, count, 0)
+        other = lax.dynamic_slice_in_dim(rows, (1 - low) * count, count, 0)
+        return mine + sent(other, OTHER_HALF)
+
     swap_b = sent(next_b, OTHER_CORE)
     last = tile(jnp.concatenate([next_b, swap_b], axis=1))
     last = over_samp(last.reshape(2 * ZS, -1, TILE))
-    return assemble(even, early[:, :TILE], early[:, TILE:], mid[:, :half], mid[:, half:], last)
+    early = pair_sum(early)
+    mid = pair_sum(mid)
+    return assembled(even, early, mid, last.astype(jnp.float32).sum(0))
 
 
 def solution(mesh):

time: 140 us -> 149 us (1.064)
  the two profiles are of different devices: /device:TPU:24 before, /device:TPU:32 now
where the time goes in v3:
time: 149 us; the launch traced here: 148 us
  waiting for transfers between devices  68 us (46%)
  starting transfers between devices  36.8 us (25%)
  blocking collectives  20.8 us (14%)
  other arithmetic  10.1 us (7%)
  matrix products  9.6 us (6%)
  local copies, waits for them, and re-layouts  2.64 us (2%)
    ppermute x8, waiting for transfers between devices, sent(): return lax.ppermute(value, AXES, pairs)  32.6 us
    all_to_all x2, waiting for transfers between devices, over_z(): lax.all_to_all(value, 'samp', 0, 0, tiled=True, axis_index_groups=Z_GROUPS)  28.3 us
    ppermute x8, starting transfers between devices, sent(): return lax.ppermute(value, AXES, pairs)  26.1 us
    all_to_all x1, blocking collectives, over_samp(): return lax.all_to_all(value, 'samp', 0, 0, tiled=True)  20.8 us
    dot_general x4, matrix products, tile(): lax.dot_general(scaled, panel, (((0,), (0,)), ((), ())), preferred_elemen...  9.6 us
    all_to_all x1, waiting for transfers between devices, over_samp(): return lax.all_to_all(value, 'samp', 0, 0, tiled=True)  7.06 us
    all_to_all x2, starting transfers between devices, over_z(): lax.all_to_all(value, 'samp', 0, 0, tiled=True, axis_index_groups=Z_GROUPS)  7.05 us
    convert_element_type x2, other arithmetic, standardized(): (observed * (observed * raw - stats[0]) * stats[1]).astype(jnp.bfloat16)  4.17 us
  transfers between devices with their start and end apart: 11, of which 8 were waited for; matrix products, arithmetic and copies ran while one was open for 11% of the time, Pallas kernels for 0%

profile of v3, /device:TPU:32, one launch (start us, length us, event | category | flops | bytes accessed | tf_op | source)
XLA Modules:
  0.0 148.2 jit_solution(14049103547829951654)
XLA Ops:
  0.0 2.7 %fusion.5 = (f32[512]{0:T(512)S(1)}, f32[512]{0:T(512)S(1)}, f32[512]{0:T(512)S(1)}) fusion(bf16[2048,512]{1,0:T(8,128)(2,1)} %param.1), kind=kLoop, calls=%fused_computation.9 | loop fusion | flops 8387072 | bytes 2103296 | tf_op jit(solution)/shard_map/reduce_sum | solution.py:83
  2.7 20.8 %all_to_all.20 = f32[16,3,512]{2,1,0:T(4,128)S(1)} all-to-all(f32[16,3,512]{2,1,0:T(4,128)S(1)} %broadcast_in_dim.2), channel_id=1, replica_groups=mesh['band'=32,'samp'=16] {'samp'}, dimensions={0} | all-to-all | bytes 196608 | tf_op jit(solution)/shard_map/all_to_all | solution.py:45
  23.6 1.7 %fusion.14 = bf16[2048,256]{1,0:T(8,128)(2,1)S(1)} fusion(f32[256]{0:T(256)S(1)} %bitcast.26, f32[256]{0:T(256)S(1)} %bitcast.25, bf16[2048,512]{1,0:T(8,128)(2,1)} %param.1), kind=kLoop, calls=%fused_computation.20 | loop fusion | flops 3670016 | bytes 2099200 | tf_op jit(solution)/shard_map/convert_element_type | solution.py:51
  25.3 4.5 %collective-permute-start.3 = (bf16[2048,256]{1,0:T(8,128)(2,1)S(1)}, bf16[2048,256]{1,0:T(8,128)(2,1)S(1)}, u32[]{:S(2)}, u32[]{:S(2)}) collective-permute-start(bf16[2048,256]{1,0:T(8,128)(2,1)S(1)} %fusion.14), channel_id=1, source_target_pairs={{32,0},{48,16},{34,2},{50,18},{36,4},{52,20},{38,6},{54,22},{40,8}... | collective-permute-start | bytes 3145736 | tf_op jit(solution)/shard_map/ppermute | solution.py:37
  29.8 1.9 %collective-permute-start = (bf16[2048,512]{1,0:T(8,128)(2,1)}, bf16[2048,512]{1,0:T(8,128)(2,1)}, u32[]{:S(2)}, u32[]{:S(2)}) collective-permute-start(bf16[2048,512]{1,0:T(8,128)(2,1)} %param.1), channel_id=1, source_target_pairs={{16,0},{18,2},{20,4},{22,6},{24,8},{26,10},{28,12},{30,14},{17,1},... | collective-permute-start | bytes 6291464 | tf_op jit(solution)/shard_map/ppermute | solution.py:37
  31.7 20.4 %collective-permute-done.3 = bf16[2048,256]{1,0:T(8,128)(2,1)S(1)} collective-permute-done((bf16[2048,256]{1,0:T(8,128)(2,1)S(1)}, bf16[2048,256]{1,0:T(8,128)(2,1)S(1)}, u32[]{:S(2)}, u32[]{:S(2)}) %collective-permute-start.3) | collective-permute-done | bytes 1048608 | tf_op jit(solution)/shard_map/ppermute | solution.py:37
  52.1 1.9 %collective-permute-start.4 = (bf16[2048,256]{1,0:T(8,128)(2,1)S(1)}, bf16[2048,256]{1,0:T(8,128)(2,1)S(1)}, u32[]{:S(2)}, u32[]{:S(2)}) collective-permute-start(bf16[2048,256]{1,0:T(8,128)(2,1)S(1)} %collective-permute-done.3), channel_id=1, source_target_pairs={{0,16},{16,0},{2,18},{18,2},{4,20},{20,4},{6,22},{22,6},{8,24},{24... | collective-permute-start | bytes 3145736 | tf_op jit(solution)/shard_map/ppermute | solution.py:37
  54.0 2.5 %fusion.7 = bf16[2048,512]{1,0:T(8,128)(2,1)S(1)} fusion(bf16[2048,512]{1,0:T(8,128)(2,1)} %param.1, f32[512]{0:T(512)S(1)} %bitcast.20, f32[512]{0:T(512)S(1)} %bitcast.21), kind=kLoop, calls=%fused_computation.11 | loop fusion | flops 7340032 | bytes 4198400 | tf_op jit(solution)/shard_map/convert_element_type | solution.py:51
  56.6 2.5 %collective-permute-start.1 = (f32[2,512]{1,0:T(2,128)S(1)}, f32[2,512]{1,0:T(2,128)S(1)}, u32[]{:S(2)}, u32[]{:S(2)}) collective-permute-start(f32[2,512]{1,0:T(2,128)S(1)} %pad_maximum_fusion.2), channel_id=1, source_target_pairs={{16,0},{18,2},{20,4},{22,6},{24,8},{26,10},{28,12},{30,14},{17,1},... | collective-permute-start | bytes 12296 | tf_op jit(solution)/shard_map/ppermute | solution.py:37
  59.0 1.1 slice.68
  60.1 6.1 %collective-permute-start.6 = (bf16[2048,256]{1,0:T(8,128)(2,1)}, bf16[2048,256]{1,0:T(8,128)(2,1)}, u32[]{:S(2)}, u32[]{:S(2)}) collective-permute-start(bf16[2048,256]{1,0:T(8,128)(2,1)} %slice.68), channel_id=1, source_target_pairs={{32,0},{48,16},{34,2},{50,18},{36,4},{52,20},{38,6},{54,22},{40,8}... | collective-permute-start | bytes 3145736 | tf_op jit(solution)/shard_map/ppermute | solution.py:37
  66.2 1.3 fusion.40
  67.5 0.0 collective-permute-done.4
  67.5 2.1 %fusion.41 = bf16[512,512]{1,0:T(8,128)(2,1)} fusion(bf16[2048,512]{1,0:T(8,128)(2,1)S(1)} %fusion.7, bf16[2048,256]{1,0:T(8,128)(2,1)S(1)} %collective-permute-done.4, bf16[2048,256]{1,0:T(8,128)(2,1)S(1)} %collective-permute-done.3), kind=kOutput, calls=%fused_computation.40 | convolution fusion | flops 1078460416 | bytes 4718592 | tf_op jit(solution)/shard_map/dot_general | solution.py:96
  69.5 3.5 %all-to-all-start.2 = ((bf16[8,64,512]{2,1,0:T(8,128)(2,1)}), bf16[8,64,512]{2,1,0:T(8,128)(2,1)S(1)}, u32[]{:S(2)}, u32[]{:S(2)}) async-start(bf16[8,64,512]{2,1,0:T(8,128)(2,1)} %bitcast.19), calls=%async_computation.2 | async-start | bytes 1048576 | tf_op jit(solution)/shard_map/all_to_all | solution.py:41
  73.0 6.5 %collective-permute-done.1 = f32[2,512]{1,0:T(2,128)S(1)} collective-permute-done((f32[2,512]{1,0:T(2,128)S(1)}, f32[2,512]{1,0:T(2,128)S(1)}, u32[]{:S(2)}, u32[]{:S(2)}) %collective-permute-start.1) | collective-permute-done | bytes 4128 | tf_op jit(solution)/shard_map/ppermute | solution.py:37
  79.6 0.0 collective-permute-done
  79.6 2.9 %fusion.37 = bf16[512,512]{1,0:T(8,128)(2,1)S(1)} fusion(bf16[2048,512]{1,0:T(8,128)(2,1)S(1)} %fusion.7, bf16[2048,512]{1,0:T(8,128)(2,1)} %collective-permute-done, f32[512]{0:T(512)S(1)} %bitcast.28, f32[512]{0:T(512)S(1)} %bitcast.27), kind=kOutput, calls=%fused_computation.38 | convolution fusion | flops 1081606144 | bytes 4722688 | tf_op jit(solution)/shard_map/dot_general | solution.py:96
  82.5 1.1 pad_maximum_fusion
  83.7 7.5 %all-to-all-done.2 = bf16[8,64,512]{2,1,0:T(8,128)(2,1)S(1)} async-done(((bf16[8,64,512]{2,1,0:T(8,128)(2,1)}), bf16[8,64,512]{2,1,0:T(8,128)(2,1)S(1)}, u32[]{:S(2)}, u32[]{:S(2)}) %all-to-all-start.2) | async-done | bytes 524320 | tf_op jit(solution)/shard_map/all_to_all | solution.py:41
  91.2 0.0 copy-start
  91.2 0.8 copy-done
  92.0 3.6 %all-to-all-start.1 = ((bf16[8,64,1024]{2,1,0:T(8,128)(2,1)}), bf16[8,64,1024]{2,1,0:T(8,128)(2,1)S(1)}, u32[]{:S(2)}, u32[]{:S(2)}) async-start(bf16[8,64,1024]{2,1,0:T(8,128)(2,1)} %bitcast.17), calls=%async_computation.1 | async-start | bytes 2097152 | tf_op jit(solution)/shard_map/all_to_all | solution.py:41
  95.5 0.3 collective-permute-done.6
  95.9 1.9 %collective-permute-start.7 = (bf16[2048,256]{1,0:T(8,128)(2,1)}, bf16[2048,256]{1,0:T(8,128)(2,1)S(1)}, u32[]{:S(2)}, u32[]{:S(2)}) collective-permute-start(bf16[2048,256]{1,0:T(8,128)(2,1)} %collective-permute-done.6), channel_id=1, source_target_pairs={{0,16},{16,0},{2,18},{18,2},{4,20},{20,4},{6,22},{22,6},{8,24},{24... | collective-permute-start | bytes 3145736 | tf_op jit(solution)/shard_map/ppermute | solution.py:37
  97.8 2.8 %collective-permute-done.7 = bf16[2048,256]{1,0:T(8,128)(2,1)S(1)} collective-permute-done((bf16[2048,256]{1,0:T(8,128)(2,1)}, bf16[2048,256]{1,0:T(8,128)(2,1)S(1)}, u32[]{:S(2)}, u32[]{:S(2)}) %collective-permute-start.7) | collective-permute-done | bytes 1048608 | tf_op jit(solution)/shard_map/ppermute | solution.py:37
  100.6 3.3 %fusion.44 = bf16[512,512]{1,0:T(8,128)(2,1)} fusion(bf16[2048,512]{1,0:T(8,128)(2,1)S(1)} %fusion.7, bf16[2048,256]{1,0:T(8,128)(2,1)S(1)} %collective-permute-done.7, bf16[2048,256]{1,0:T(8,128)(2,1)} %collective-permute-done.6), kind=kOutput, calls=%fused_computation.41 | convolution fusion | flops 1078460416 | bytes 4718592 | tf_op jit(solution)/shard_map/dot_general | solution.py:96
  103.9 20.8 %all-to-all-done.1 = bf16[8,64,1024]{2,1,0:T(8,128)(2,1)S(1)} async-done(((bf16[8,64,1024]{2,1,0:T(8,128)(2,1)}), bf16[8,64,1024]{2,1,0:T(8,128)(2,1)S(1)}, u32[]{:S(2)}, u32[]{:S(2)}) %all-to-all-start.1) | async-done | bytes 1048608 | tf_op jit(solution)/shard_map/all_to_all | solution.py:41
  124.7 3.6 %all-to-all-start.3 = ((bf16[16,32,512]{2,1,0:T(8,128)(2,1)}), bf16[16,32,512]{2,1,0:T(8,128)(2,1)S(1)}, u32[]{:S(2)}, u32[]{:S(2)}) async-start(bf16[16,32,512]{2,1,0:T(8,128)(2,1)} %bitcast.18), calls=%async_computation.3 | async-start | bytes 1048576 | tf_op jit(solution)/shard_map/all_to_all | solution.py:45
  128.3 1.1 convert_reduce_fusion.2
  129.5 3.7 %collective-permute-start.5 = (f32[32,512]{1,0:T(8,128)S(1)}, f32[32,512]{1,0:T(8,128)S(1)}, u32[]{:S(2)}, u32[]{:S(2)}) collective-permute-start(f32[32,512]{1,0:T(8,128)S(1)} %constant_dynamic-slice_fusion), channel_id=1, source_target_pairs={{0,1},{16,17},{2,3},{18,19},{4,5},{20,21},{6,7},{22,23},{8,9},{24,... | collective-permute-start | bytes 196616 | tf_op jit(solution)/shard_map/ppermute | solution.py:37
  133.2 2.5 %collective-permute-done.5 = f32[32,512]{1,0:T(8,128)S(1)} collective-permute-done((f32[32,512]{1,0:T(8,128)S(1)}, f32[32,512]{1,0:T(8,128)S(1)}, u32[]{:S(2)}, u32[]{:S(2)}) %collective-permute-start.5) | collective-permute-done | bytes 65568 | tf_op jit(solution)/shard_map/ppermute | solution.py:37
  135.7 0.2 convert_reduce_fusion
  135.9 3.6 %collective-permute-start.2 = (f32[32,1024]{1,0:T(8,128)S(1)}, f32[32,1024]{1,0:T(8,128)S(1)}, u32[]{:S(2)}, u32[]{:S(2)}) collective-permute-start(f32[32,1024]{1,0:T(8,128)S(1)} %constant_dynamic-slice_fusion.1), channel_id=1, source_target_pairs={{0,1},{16,17},{2,3},{18,19},{4,5},{20,21},{6,7},{22,23},{8,9},{24,... | collective-permute-start | bytes 393224 | tf_op jit(solution)/shard_map/ppermute | solution.py:37
  139.6 7.1 %all-to-all-done.3 = bf16[16,32,512]{2,1,0:T(8,128)(2,1)S(1)} async-done(((bf16[16,32,512]{2,1,0:T(8,128)(2,1)}), bf16[16,32,512]{2,1,0:T(8,128)(2,1)S(1)}, u32[]{:S(2)}, u32[]{:S(2)}) %all-to-all-start.3) | async-done | bytes 524320 | tf_op jit(solution)/shard_map/all_to_all | solution.py:45
  146.6 0.1 convert_reduce_fusion.1
  146.7 0.0 collective-permute-done.2
  146.8 0.0 copy-start.1
  146.9 0.7 copy-done.1
  147.5 0.6 select_dynamic-update-slice_fusion
  (18 shorter events, 0.2 us)
Async XLA Ops:
  25.3 26.9 %collective-permute-start.3 = (bf16[2048,256]{1,0:T(8,128)(2,1)S(1)}, bf16[2048,256]{1,0:T(8,128)(2,1)S(1)}, u32[]{:S(2)}, u32[]{:S(2)}) collective-permute-start(bf16[2048,256]{1,0:T(8,128)(2,1)S(1)} %fusion.14), channel_id=1, source_target_pairs={{32,0},{48,16},{34,2},{50,18},{36,4},{52,20},{38,6},{54,22},{40,8}... | collective-permute-start | bytes 3145736 | tf_op jit(solution)/shard_map/ppermute | solution.py:37
  29.8 49.8 %collective-permute-start = (bf16[2048,512]{1,0:T(8,128)(2,1)}, bf16[2048,512]{1,0:T(8,128)(2,1)}, u32[]{:S(2)}, u32[]{:S(2)}) collective-permute-start(bf16[2048,512]{1,0:T(8,128)(2,1)} %param.1), channel_id=1, source_target_pairs={{16,0},{18,2},{20,4},{22,6},{24,8},{26,10},{28,12},{30,14},{17,1},... | collective-permute-start | bytes 6291464 | tf_op jit(solution)/shard_map/ppermute | solution.py:37
  52.1 15.3 %collective-permute-start.4 = (bf16[2048,256]{1,0:T(8,128)(2,1)S(1)}, bf16[2048,256]{1,0:T(8,128)(2,1)S(1)}, u32[]{:S(2)}, u32[]{:S(2)}) collective-permute-start(bf16[2048,256]{1,0:T(8,128)(2,1)S(1)} %collective-permute-done.3), channel_id=1, source_target_pairs={{0,16},{16,0},{2,18},{18,2},{4,20},{20,4},{6,22},{22,6},{8,24},{24... | collective-permute-start | bytes 3145736 | tf_op jit(solution)/shard_map/ppermute | solution.py:37
  56.6 23.0 %collective-permute-start.1 = (f32[2,512]{1,0:T(2,128)S(1)}, f32[2,512]{1,0:T(2,128)S(1)}, u32[]{:S(2)}, u32[]{:S(2)}) collective-permute-start(f32[2,512]{1,0:T(2,128)S(1)} %pad_maximum_fusion.2), channel_id=1, source_target_pairs={{16,0},{18,2},{20,4},{22,6},{24,8},{26,10},{28,12},{30,14},{17,1},... | collective-permute-start | bytes 12296 | tf_op jit(solution)/shard_map/ppermute | solution.py:37
  60.1 35.8 %collective-permute-start.6 = (bf16[2048,256]{1,0:T(8,128)(2,1)}, bf16[2048,256]{1,0:T(8,128)(2,1)}, u32[]{:S(2)}, u32[]{:S(2)}) collective-permute-start(bf16[2048,256]{1,0:T(8,128)(2,1)} %slice.68), channel_id=1, source_target_pairs={{32,0},{48,16},{34,2},{50,18},{36,4},{52,20},{38,6},{54,22},{40,8}... | collective-permute-start | bytes 3145736 | tf_op jit(solution)/shard_map/ppermute | solution.py:37
  69.5 21.6 %all-to-all-start.2 = ((bf16[8,64,512]{2,1,0:T(8,128)(2,1)}), bf16[8,64,512]{2,1,0:T(8,128)(2,1)S(1)}, u32[]{:S(2)}, u32[]{:S(2)}) async-start(bf16[8,64,512]{2,1,0:T(8,128)(2,1)} %bitcast.19), calls=%async_computation.2 | async-start | bytes 1048576 | tf_op jit(solution)/shard_map/all_to_all | solution.py:41
  91.2 0.8 copy-start
  92.0 32.7 %all-to-all-start.1 = ((bf16[8,64,1024]{2,1,0:T(8,128)(2,1)}), bf16[8,64,1024]{2,1,0:T(8,128)(2,1)S(1)}, u32[]{:S(2)}, u32[]{:S(2)}) async-start(bf16[8,64,1024]{2,1,0:T(8,128)(2,1)} %bitcast.17), calls=%async_computation.1 | async-start | bytes 2097152 | tf_op jit(solution)/shard_map/all_to_all | solution.py:41
  95.9 4.8 %collective-permute-start.7 = (bf16[2048,256]{1,0:T(8,128)(2,1)}, bf16[2048,256]{1,0:T(8,128)(2,1)S(1)}, u32[]{:S(2)}, u32[]{:S(2)}) collective-permute-start(bf16[2048,256]{1,0:T(8,128)(2,1)} %collective-permute-done.6), channel_id=1, source_target_pairs={{0,16},{16,0},{2,18},{18,2},{4,20},{20,4},{6,22},{22,6},{8,24},{24... | collective-permute-start | bytes 3145736 | tf_op jit(solution)/shard_map/ppermute | solution.py:37
  124.7 21.9 %all-to-all-start.3 = ((bf16[16,32,512]{2,1,0:T(8,128)(2,1)}), bf16[16,32,512]{2,1,0:T(8,128)(2,1)S(1)}, u32[]{:S(2)}, u32[]{:S(2)}) async-start(bf16[16,32,512]{2,1,0:T(8,128)(2,1)} %bitcast.18), calls=%async_computation.3 | async-start | bytes 1048576 | tf_op jit(solution)/shard_map/all_to_all | solution.py:45
  129.5 6.3 %collective-permute-start.5 = (f32[32,512]{1,0:T(8,128)S(1)}, f32[32,512]{1,0:T(8,128)S(1)}, u32[]{:S(2)}, u32[]{:S(2)}) collective-permute-start(f32[32,512]{1,0:T(8,128)S(1)} %constant_dynamic-slice_fusion), channel_id=1, source_target_pairs={{0,1},{16,17},{2,3},{18,19},{4,5},{20,21},{6,7},{22,23},{8,9},{24,... | collective-permute-start | bytes 196616 | tf_op jit(solution)/shard_map/ppermute | solution.py:37
  135.9 10.8 %collective-permute-start.2 = (f32[32,1024]{1,0:T(8,128)S(1)}, f32[32,1024]{1,0:T(8,128)S(1)}, u32[]{:S(2)}, u32[]{:S(2)}) collective-permute-start(f32[32,1024]{1,0:T(8,128)S(1)} %constant_dynamic-slice_fusion.1), channel_id=1, source_target_pairs={{0,1},{16,17},{2,3},{18,19},{4,5},{20,21},{6,7},{22,23},{8,9},{24,... | collective-permute-start | bytes 393224 | tf_op jit(solution)/shard_map/ppermute | solution.py:37
  146.8 0.7 copy-start.1

commit v4 on v3

--- a/solution.py
+++ b/solution.py
@@ -6,6 +6,7 @@
 
 
 TILE = 512
+WIN = 2048
 AXES = ("band", "samp")
 YS, XS, ZS, CORES = 8, 4, 8, 2
 
@@ -53,21 +54,27 @@
 
 def assembled(even, early, mid, last):
     half = mid.shape[1] // 2
-    own, edge = early[:, :TILE], early[:, TILE:]
-    low, high, next_low, next_high = mid[:, half:], last[:, half:], mid[:, :half], last[:, :half]
-    edge_low, edge_high = edge[:, :half], edge[:, half:]
-    return jnp.concatenate(
-        [
-            own,
-            jnp.where(even, edge_low, low),
-            jnp.where(even, edge_high, high),
-            next_low,
-            next_high,
-            jnp.where(even, low, edge_low),
-            jnp.where(even, high, edge_high),
-        ],
-        axis=1,
-    )
+    own, edge, low = early[:, :TILE], early[:, TILE:], mid[:, half:]
+    high, none = edge[:, half:], jnp.zeros_like(low)
+    swapped_at_3 = [jnp.where(even, edge[:, :half], low), jnp.where(even, high, none)]
+    swapped_at_1 = [jnp.where(even, low, edge[:, :half]), jnp.where(even, none, high)]
+    base = jnp.concatenate([own, *swapped_at_3, mid[:, :half], none, *swapped_at_1], axis=1)
+    base, last = lax.optimization_barrier((base, last))
+
+    def placed(value, start):
+        return jnp.pad(value, ((0, 0), (start, WIN - start - value.shape[1])))
+
+    at_1, at_3 = (placed(last[:, half:], t * TILE + half) for t in (1, 3))
+    return base + placed(last[:, :half], 2 * TILE + half) + jnp.where(even, at_3, at_1)
+
+
+def widened(value, width):
+    return lax.optimization_barrier(jnp.pad(value, ((0, 0), (0, width))))
+
+
+def filled(wide, value):
+    start = wide.shape[1] - value.shape[1]
+    return lax.optimization_barrier(lax.dynamic_update_slice(wide, value, (0, start)))
 
 
 def on_device(dosage):
@@ -104,7 +111,7 @@
     early = jnp.concatenate([own, edge], axis=1)
     early = over_z(early.reshape(ZS, -1, 2 * TILE)).astype(jnp.float32).sum(0)
     swap_a = sent(next_a, OTHER_CORE)
-    mid = tile(jnp.concatenate([next_a, swap_a], axis=1))
+    mid = tile(filled(widened(next_a, half), swap_a))
     mid = over_z(mid.reshape(ZS, -1, TILE)).astype(jnp.float32).sum(0)
     count = early.shape[0] // 2
 
@@ -114,7 +121,7 @@
         return mine + sent(other, OTHER_HALF)
 
     swap_b = sent(next_b, OTHER_CORE)
-    last = tile(jnp.concatenate([next_b, swap_b], axis=1))
+    last = tile(filled(widened(next_b, half), swap_b))
     last = over_samp(last.reshape(2 * ZS, -1, TILE))
     early = pair_sum(early)
     mid = pair_sum(mid)

time: 149 us -> 149 us (level)
    ppermute x8, waiting for transfers between devices: 32.6 us -> 30.8 us  [sent(): return lax.ppermute(value, AXES, pairs)]
    all_to_all x2, waiting for transfers between devices: 28.3 us -> 29.9 us  [over_z(): lax.all_to_all(value, 'samp', 0, 0, tiled=True, axis_index_groups=Z_GROUPS)]
    pad x0 -> x2, local copies, waits for them, and re-layouts: none -> 1.51 us  [widened(): return lax.optimization_barrier(jnp.pad(value, ((0, 0), (0, width))))]
where the time goes in v4:
time: 149 us; the launch traced here: 148 us
  waiting for transfers between devices  67.7 us (45%)
  starting transfers between devices  36.8 us (25%)
  blocking collectives  20.8 us (14%)
  other arithmetic  10.2 us (7%)
  matrix products  8.37 us (6%)
  local copies, waits for them, and re-layouts  3.62 us (2%)
    ppermute x8, waiting for transfers between devices, sent(): return lax.ppermute(value, AXES, pairs)  30.8 us
    all_to_all x2, waiting for transfers between devices, over_z(): lax.all_to_all(value, 'samp', 0, 0, tiled=True, axis_index_groups=Z_GROUPS)  29.9 us
    ppermute x8, starting transfers between devices, sent(): return lax.ppermute(value, AXES, pairs)  26.1 us
    all_to_all x1, blocking collectives, over_samp(): return lax.all_to_all(value, 'samp', 0, 0, tiled=True)  20.8 us
    dot_general x4, matrix products, tile(): lax.dot_general(scaled, panel, (((0,), (0,)), ((), ())), preferred_elemen...  8.37 us
    all_to_all x1, waiting for transfers between devices, over_samp(): return lax.all_to_all(value, 'samp', 0, 0, tiled=True)  7.06 us
    all_to_all x2, starting transfers between devices, over_z(): lax.all_to_all(value, 'samp', 0, 0, tiled=True, axis_index_groups=Z_GROUPS)  7.05 us
    convert_element_type x2, other arithmetic, standardized(): (observed * (observed * raw - stats[0]) * stats[1]).astype(jnp.bfloat16)  4.17 us
  transfers between devices with their start and end apart: 11, of which 8 were waited for; matrix products, arithmetic and copies ran while one was open for 11% of the time, Pallas kernels for 0%

profile of v4, /device:TPU:32, one launch (start us, length us, event | category | flops | bytes accessed | tf_op | source)
XLA Modules:
  0.0 147.8 jit_solution(6084455631326939400)
XLA Ops:
  0.0 2.7 %fusion.5 = (f32[512]{0:T(512)S(1)}, f32[512]{0:T(512)S(1)}, f32[512]{0:T(512)S(1)}) fusion(bf16[2048,512]{1,0:T(8,128)(2,1)} %param.1), kind=kLoop, calls=%fused_computation.9 | loop fusion | flops 8387072 | bytes 2103296 | tf_op jit(solution)/shard_map/reduce_sum | solution.py:90
  2.7 20.8 %all_to_all.20 = f32[16,3,512]{2,1,0:T(4,128)S(1)} all-to-all(f32[16,3,512]{2,1,0:T(4,128)S(1)} %broadcast_in_dim.4), channel_id=1, replica_groups=mesh['band'=32,'samp'=16] {'samp'}, dimensions={0} | all-to-all | bytes 196608 | tf_op jit(solution)/shard_map/all_to_all | solution.py:46
  23.6 1.7 %fusion.14 = bf16[2048,256]{1,0:T(8,128)(2,1)S(1)} fusion(f32[256]{0:T(256)S(1)} %bitcast.27, f32[256]{0:T(256)S(1)} %bitcast.26, bf16[2048,512]{1,0:T(8,128)(2,1)} %param.1), kind=kLoop, calls=%fused_computation.20 | loop fusion | flops 3670016 | bytes 2099200 | tf_op jit(solution)/shard_map/convert_element_type | solution.py:52
  25.3 4.5 %collective-permute-start.3 = (bf16[2048,256]{1,0:T(8,128)(2,1)S(1)}, bf16[2048,256]{1,0:T(8,128)(2,1)S(1)}, u32[]{:S(2)}, u32[]{:S(2)}) collective-permute-start(bf16[2048,256]{1,0:T(8,128)(2,1)S(1)} %fusion.14), channel_id=1, source_target_pairs={{32,0},{48,16},{34,2},{50,18},{36,4},{52,20},{38,6},{54,22},{40,8}... | collective-permute-start | bytes 3145736 | tf_op jit(solution)/shard_map/ppermute | solution.py:38
  29.8 1.9 %collective-permute-start = (bf16[2048,512]{1,0:T(8,128)(2,1)}, bf16[2048,512]{1,0:T(8,128)(2,1)}, u32[]{:S(2)}, u32[]{:S(2)}) collective-permute-start(bf16[2048,512]{1,0:T(8,128)(2,1)} %param.1), channel_id=1, source_target_pairs={{16,0},{18,2},{20,4},{22,6},{24,8},{26,10},{28,12},{30,14},{17,1},... | collective-permute-start | bytes 6291464 | tf_op jit(solution)/shard_map/ppermute | solution.py:38
  31.7 20.4 %collective-permute-done.3 = bf16[2048,256]{1,0:T(8,128)(2,1)S(1)} collective-permute-done((bf16[2048,256]{1,0:T(8,128)(2,1)S(1)}, bf16[2048,256]{1,0:T(8,128)(2,1)S(1)}, u32[]{:S(2)}, u32[]{:S(2)}) %collective-permute-start.3) | collective-permute-done | bytes 1048608 | tf_op jit(solution)/shard_map/ppermute | solution.py:38
  52.1 1.9 %collective-permute-start.4 = (bf16[2048,256]{1,0:T(8,128)(2,1)S(1)}, bf16[2048,256]{1,0:T(8,128)(2,1)S(1)}, u32[]{:S(2)}, u32[]{:S(2)}) collective-permute-start(bf16[2048,256]{1,0:T(8,128)(2,1)S(1)} %collective-permute-done.3), channel_id=1, source_target_pairs={{0,16},{16,0},{2,18},{18,2},{4,20},{20,4},{6,22},{22,6},{8,24},{24... | collective-permute-start | bytes 3145736 | tf_op jit(solution)/shard_map/ppermute | solution.py:38
  54.0 2.5 %fusion.7 = bf16[2048,512]{1,0:T(8,128)(2,1)S(1)} fusion(bf16[2048,512]{1,0:T(8,128)(2,1)} %param.1, f32[512]{0:T(512)S(1)} %bitcast.21, f32[512]{0:T(512)S(1)} %bitcast.22), kind=kLoop, calls=%fused_computation.11 | loop fusion | flops 7340032 | bytes 4198400 | tf_op jit(solution)/shard_map/convert_element_type | solution.py:52
  56.6 2.5 %collective-permute-start.1 = (f32[2,512]{1,0:T(2,128)S(1)}, f32[2,512]{1,0:T(2,128)S(1)}, u32[]{:S(2)}, u32[]{:S(2)}) collective-permute-start(f32[2,512]{1,0:T(2,128)S(1)} %pad_maximum_fusion.2), channel_id=1, source_target_pairs={{16,0},{18,2},{20,4},{22,6},{24,8},{26,10},{28,12},{30,14},{17,1},... | collective-permute-start | bytes 12296 | tf_op jit(solution)/shard_map/ppermute | solution.py:38
  59.0 1.1 slice.71
  60.1 6.1 %collective-permute-start.6 = (bf16[2048,256]{1,0:T(8,128)(2,1)}, bf16[2048,256]{1,0:T(8,128)(2,1)}, u32[]{:S(2)}, u32[]{:S(2)}) collective-permute-start(bf16[2048,256]{1,0:T(8,128)(2,1)} %slice.71), channel_id=1, source_target_pairs={{32,0},{48,16},{34,2},{50,18},{36,4},{52,20},{38,6},{54,22},{40,8}... | collective-permute-start | bytes 3145736 | tf_op jit(solution)/shard_map/ppermute | solution.py:38
  66.2 1.3 fusion.26
  67.5 0.1 pad.19
  67.6 0.0 collective-permute-done.4
  67.6 0.1 constant_dynamic-update-slice_fusion.2
  67.7 2.1 %fusion.27 = bf16[512,512]{1,0:T(8,128)(2,1)} fusion(bf16[2048,512]{1,0:T(8,128)(2,1)S(1)} %fusion.7, bf16[2048,512]{1,0:T(8,128)(2,1)S(1)} %constant_dynamic-update-slice_fusion.2), kind=kOutput, calls=%fused_computation.32 | convolution fusion | flops 1074266112 | bytes 4718592 | tf_op jit(solution)/shard_map/dot_general | solution.py:103
  69.8 3.5 %all-to-all-start.2 = ((bf16[8,64,512]{2,1,0:T(8,128)(2,1)}), bf16[8,64,512]{2,1,0:T(8,128)(2,1)S(1)}, u32[]{:S(2)}, u32[]{:S(2)}) async-start(bf16[8,64,512]{2,1,0:T(8,128)(2,1)} %bitcast.10), calls=%async_computation.2 | async-start | bytes 1048576 | tf_op jit(solution)/shard_map/all_to_all | solution.py:42
  73.3 6.3 %collective-permute-done.1 = f32[2,512]{1,0:T(2,128)S(1)} collective-permute-done((f32[2,512]{1,0:T(2,128)S(1)}, f32[2,512]{1,0:T(2,128)S(1)}, u32[]{:S(2)}, u32[]{:S(2)}) %collective-permute-start.1) | collective-permute-done | bytes 4128 | tf_op jit(solution)/shard_map/ppermute | solution.py:38
  79.6 0.0 collective-permute-done
  79.6 2.9 %fusion.23 = bf16[512,512]{1,0:T(8,128)(2,1)S(1)} fusion(bf16[2048,512]{1,0:T(8,128)(2,1)S(1)} %fusion.7, bf16[2048,512]{1,0:T(8,128)(2,1)} %collective-permute-done, f32[512]{0:T(512)S(1)} %bitcast.29, f32[512]{0:T(512)S(1)} %bitcast.28), kind=kOutput, calls=%fused_computation.30 | convolution fusion | flops 1081606144 | bytes 4722688 | tf_op jit(solution)/shard_map/dot_general | solution.py:103
  82.5 1.1 pad_maximum_fusion
  83.7 7.7 %all-to-all-done.2 = bf16[8,64,512]{2,1,0:T(8,128)(2,1)S(1)} async-done(((bf16[8,64,512]{2,1,0:T(8,128)(2,1)}), bf16[8,64,512]{2,1,0:T(8,128)(2,1)S(1)}, u32[]{:S(2)}, u32[]{:S(2)}) %all-to-all-start.2) | async-done | bytes 524320 | tf_op jit(solution)/shard_map/all_to_all | solution.py:42
  91.4 0.0 copy-start
  91.4 0.8 copy-done
  92.2 3.6 %all-to-all-start.1 = ((bf16[8,64,1024]{2,1,0:T(8,128)(2,1)}), bf16[8,64,1024]{2,1,0:T(8,128)(2,1)S(1)}, u32[]{:S(2)}, u32[]{:S(2)}) async-start(bf16[8,64,1024]{2,1,0:T(8,128)(2,1)} %bitcast.19), calls=%async_computation.1 | async-start | bytes 2097152 | tf_op jit(solution)/shard_map/all_to_all | solution.py:42
  95.8 0.1 collective-permute-done.6
  95.9 1.9 %collective-permute-start.7 = (bf16[2048,256]{1,0:T(8,128)(2,1)}, bf16[2048,256]{1,0:T(8,128)(2,1)S(1)}, u32[]{:S(2)}, u32[]{:S(2)}) collective-permute-start(bf16[2048,256]{1,0:T(8,128)(2,1)} %collective-permute-done.6), channel_id=1, source_target_pairs={{0,16},{16,0},{2,18},{18,2},{4,20},{20,4},{6,22},{22,6},{8,24},{24... | collective-permute-start | bytes 3145736 | tf_op jit(solution)/shard_map/ppermute | solution.py:38
  97.8 1.4 pad.20
  99.1 1.5 collective-permute-done.7
  100.6 0.1 constant_dynamic-update-slice_fusion.1
  100.7 2.1 %fusion.28 = bf16[512,512]{1,0:T(8,128)(2,1)} fusion(bf16[2048,512]{1,0:T(8,128)(2,1)S(1)} %fusion.7, bf16[2048,512]{1,0:T(8,128)(2,1)S(1)} %constant_dynamic-update-slice_fusion.1), kind=kOutput, calls=%fused_computation.33 | convolution fusion | flops 1074266112 | bytes 4718592 | tf_op jit(solution)/shard_map/dot_general | solution.py:103
  102.8 22.2 %all-to-all-done.1 = bf16[8,64,1024]{2,1,0:T(8,128)(2,1)S(1)} async-done(((bf16[8,64,1024]{2,1,0:T(8,128)(2,1)}), bf16[8,64,1024]{2,1,0:T(8,128)(2,1)S(1)}, u32[]{:S(2)}, u32[]{:S(2)}) %all-to-all-start.1) | async-done | bytes 1048608 | tf_op jit(solution)/shard_map/all_to_all | solution.py:42
  124.9 3.6 %all-to-all-start.3 = ((bf16[16,32,512]{2,1,0:T(8,128)(2,1)}), bf16[16,32,512]{2,1,0:T(8,128)(2,1)S(1)}, u32[]{:S(2)}, u32[]{:S(2)}) async-start(bf16[16,32,512]{2,1,0:T(8,128)(2,1)} %bitcast.20), calls=%async_computation.3 | async-start | bytes 1048576 | tf_op jit(solution)/shard_map/all_to_all | solution.py:46
  128.5 1.1 convert_reduce_fusion.2
  129.7 3.7 %collective-permute-start.5 = (f32[32,512]{1,0:T(8,128)S(1)}, f32[32,512]{1,0:T(8,128)S(1)}, u32[]{:S(2)}, u32[]{:S(2)}) collective-permute-start(f32[32,512]{1,0:T(8,128)S(1)} %constant_dynamic-slice_fusion), channel_id=1, source_target_pairs={{0,1},{16,17},{2,3},{18,19},{4,5},{20,21},{6,7},{22,23},{8,9},{24,... | collective-permute-start | bytes 196616 | tf_op jit(solution)/shard_map/ppermute | solution.py:38
  133.4 2.5 %collective-permute-done.5 = f32[32,512]{1,0:T(8,128)S(1)} collective-permute-done((f32[32,512]{1,0:T(8,128)S(1)}, f32[32,512]{1,0:T(8,128)S(1)}, u32[]{:S(2)}, u32[]{:S(2)}) %collective-permute-start.5) | collective-permute-done | bytes 65568 | tf_op jit(solution)/shard_map/ppermute | solution.py:38
  136.0 0.2 convert_reduce_fusion
  136.2 3.6 %collective-permute-start.2 = (f32[32,1024]{1,0:T(8,128)S(1)}, f32[32,1024]{1,0:T(8,128)S(1)}, u32[]{:S(2)}, u32[]{:S(2)}) collective-permute-start(f32[32,1024]{1,0:T(8,128)S(1)} %constant_dynamic-slice_fusion.1), channel_id=1, source_target_pairs={{0,1},{16,17},{2,3},{18,19},{4,5},{20,21},{6,7},{22,23},{8,9},{24,... | collective-permute-start | bytes 393224 | tf_op jit(solution)/shard_map/ppermute | solution.py:38
  139.8 7.1 %all-to-all-done.3 = bf16[16,32,512]{2,1,0:T(8,128)(2,1)S(1)} async-done(((bf16[16,32,512]{2,1,0:T(8,128)(2,1)}), bf16[16,32,512]{2,1,0:T(8,128)(2,1)S(1)}, u32[]{:S(2)}, u32[]{:S(2)}) %all-to-all-start.3) | async-done | bytes 524320 | tf_op jit(solution)/shard_map/all_to_all | solution.py:46
  146.9 0.1 convert_reduce_fusion.1
  146.9 0.0 collective-permute-done.2
  147.1 0.7 select_add_fusion
  (20 shorter events, 0.2 us)
Async XLA Ops:
  25.3 26.9 %collective-permute-start.3 = (bf16[2048,256]{1,0:T(8,128)(2,1)S(1)}, bf16[2048,256]{1,0:T(8,128)(2,1)S(1)}, u32[]{:S(2)}, u32[]{:S(2)}) collective-permute-start(bf16[2048,256]{1,0:T(8,128)(2,1)S(1)} %fusion.14), channel_id=1, source_target_pairs={{32,0},{48,16},{34,2},{50,18},{36,4},{52,20},{38,6},{54,22},{40,8}... | collective-permute-start | bytes 3145736 | tf_op jit(solution)/shard_map/ppermute | solution.py:38
  29.8 49.8 %collective-permute-start = (bf16[2048,512]{1,0:T(8,128)(2,1)}, bf16[2048,512]{1,0:T(8,128)(2,1)}, u32[]{:S(2)}, u32[]{:S(2)}) collective-permute-start(bf16[2048,512]{1,0:T(8,128)(2,1)} %param.1), channel_id=1, source_target_pairs={{16,0},{18,2},{20,4},{22,6},{24,8},{26,10},{28,12},{30,14},{17,1},... | collective-permute-start | bytes 6291464 | tf_op jit(solution)/shard_map/ppermute | solution.py:38
  52.1 15.5 %collective-permute-start.4 = (bf16[2048,256]{1,0:T(8,128)(2,1)S(1)}, bf16[2048,256]{1,0:T(8,128)(2,1)S(1)}, u32[]{:S(2)}, u32[]{:S(2)}) collective-permute-start(bf16[2048,256]{1,0:T(8,128)(2,1)S(1)} %collective-permute-done.3), channel_id=1, source_target_pairs={{0,16},{16,0},{2,18},{18,2},{4,20},{20,4},{6,22},{22,6},{8,24},{24... | collective-permute-start | bytes 3145736 | tf_op jit(solution)/shard_map/ppermute | solution.py:38
  56.6 23.0 %collective-permute-start.1 = (f32[2,512]{1,0:T(2,128)S(1)}, f32[2,512]{1,0:T(2,128)S(1)}, u32[]{:S(2)}, u32[]{:S(2)}) collective-permute-start(f32[2,512]{1,0:T(2,128)S(1)} %pad_maximum_fusion.2), channel_id=1, source_target_pairs={{16,0},{18,2},{20,4},{22,6},{24,8},{26,10},{28,12},{30,14},{17,1},... | collective-permute-start | bytes 12296 | tf_op jit(solution)/shard_map/ppermute | solution.py:38
  60.1 35.8 %collective-permute-start.6 = (bf16[2048,256]{1,0:T(8,128)(2,1)}, bf16[2048,256]{1,0:T(8,128)(2,1)}, u32[]{:S(2)}, u32[]{:S(2)}) collective-permute-start(bf16[2048,256]{1,0:T(8,128)(2,1)} %slice.71), channel_id=1, source_target_pairs={{32,0},{48,16},{34,2},{50,18},{36,4},{52,20},{38,6},{54,22},{40,8}... | collective-permute-start | bytes 3145736 | tf_op jit(solution)/shard_map/ppermute | solution.py:38
  69.8 21.6 %all-to-all-start.2 = ((bf16[8,64,512]{2,1,0:T(8,128)(2,1)}), bf16[8,64,512]{2,1,0:T(8,128)(2,1)S(1)}, u32[]{:S(2)}, u32[]{:S(2)}) async-start(bf16[8,64,512]{2,1,0:T(8,128)(2,1)} %bitcast.10), calls=%async_computation.2 | async-start | bytes 1048576 | tf_op jit(solution)/shard_map/all_to_all | solution.py:42
  91.4 0.8 copy-start
  92.2 32.7 %all-to-all-start.1 = ((bf16[8,64,1024]{2,1,0:T(8,128)(2,1)}), bf16[8,64,1024]{2,1,0:T(8,128)(2,1)S(1)}, u32[]{:S(2)}, u32[]{:S(2)}) async-start(bf16[8,64,1024]{2,1,0:T(8,128)(2,1)} %bitcast.19), calls=%async_computation.1 | async-start | bytes 2097152 | tf_op jit(solution)/shard_map/all_to_all | solution.py:42
  95.9 4.8 %collective-permute-start.7 = (bf16[2048,256]{1,0:T(8,128)(2,1)}, bf16[2048,256]{1,0:T(8,128)(2,1)S(1)}, u32[]{:S(2)}, u32[]{:S(2)}) collective-permute-start(bf16[2048,256]{1,0:T(8,128)(2,1)} %collective-permute-done.6), channel_id=1, source_target_pairs={{0,16},{16,0},{2,18},{18,2},{4,20},{20,4},{6,22},{22,6},{8,24},{24... | collective-permute-start | bytes 3145736 | tf_op jit(solution)/shard_map/ppermute | solution.py:38
  124.9 21.9 %all-to-all-start.3 = ((bf16[16,32,512]{2,1,0:T(8,128)(2,1)}), bf16[16,32,512]{2,1,0:T(8,128)(2,1)S(1)}, u32[]{:S(2)}, u32[]{:S(2)}) async-start(bf16[16,32,512]{2,1,0:T(8,128)(2,1)} %bitcast.20), calls=%async_computation.3 | async-start | bytes 1048576 | tf_op jit(solution)/shard_map/all_to_all | solution.py:46
  129.7 6.3 %collective-permute-start.5 = (f32[32,512]{1,0:T(8,128)S(1)}, f32[32,512]{1,0:T(8,128)S(1)}, u32[]{:S(2)}, u32[]{:S(2)}) collective-permute-start(f32[32,512]{1,0:T(8,128)S(1)} %constant_dynamic-slice_fusion), channel_id=1, source_target_pairs={{0,1},{16,17},{2,3},{18,19},{4,5},{20,21},{6,7},{22,23},{8,9},{24,... | collective-permute-start | bytes 196616 | tf_op jit(solution)/shard_map/ppermute | solution.py:38
  136.2 10.8 %collective-permute-start.2 = (f32[32,1024]{1,0:T(8,128)S(1)}, f32[32,1024]{1,0:T(8,128)S(1)}, u32[]{:S(2)}, u32[]{:S(2)}) collective-permute-start(f32[32,1024]{1,0:T(8,128)S(1)} %constant_dynamic-slice_fusion.1), channel_id=1, source_target_pairs={{0,1},{16,17},{2,3},{18,19},{4,5},{20,21},{6,7},{22,23},{8,9},{24,... | collective-permute-start | bytes 393224 | tf_op jit(solution)/shard_map/ppermute | solution.py:38

commit v5 on v4

--- a/solution.py
+++ b/solution.py
@@ -7,6 +7,7 @@
 
 TILE = 512
 WIN = 2048
+EDGE_FIRST = 384
 AXES = ("band", "samp")
 YS, XS, ZS, CORES = 8, 4, 8, 2
 
@@ -107,12 +108,15 @@
         return with_layout_constraint(product, Layout(major_to_minor=(0, 1)))
 
     own = tile(scaled)
-    edge = tile(standardized(edge_raw, edge_stats))
+    edge_rest = lax.optimization_barrier(
+        standardized(edge_raw[:, EDGE_FIRST:], edge_stats[:, EDGE_FIRST:])
+    )
+    edge = tile(standardized(edge_raw[:, :EDGE_FIRST], edge_stats[:, :EDGE_FIRST]))
     early = jnp.concatenate([own, edge], axis=1)
-    early = over_z(early.reshape(ZS, -1, 2 * TILE)).astype(jnp.float32).sum(0)
+    early = over_z(early.reshape(ZS, -1, TILE + EDGE_FIRST)).astype(jnp.float32).sum(0)
     swap_a = sent(next_a, OTHER_CORE)
-    mid = tile(filled(widened(next_a, half), swap_a))
-    mid = over_z(mid.reshape(ZS, -1, TILE)).astype(jnp.float32).sum(0)
+    mid = tile(filled(widened(jnp.concatenate([next_a, edge_rest], axis=1), half), swap_a))
+    mid = over_z(mid.reshape(ZS, -1, mid.shape[1])).astype(jnp.float32).sum(0)
     count = early.shape[0] // 2
 
     def pair_sum(rows):
@@ -125,6 +129,9 @@
     last = over_samp(last.reshape(2 * ZS, -1, TILE))
     early = pair_sum(early)
     mid = pair_sum(mid)
+    rest_at = half + TILE - EDGE_FIRST
+    early = jnp.concatenate([early, mid[:, half:rest_at]], axis=1)
+    mid = jnp.concatenate([mid[:, :half], mid[:, rest_at:]], axis=1)
     return assembled(even, early, mid, last.astype(jnp.float32).sum(0))
 
 

time: 149 us -> 181 us (1.21)
  the two profiles are of different devices: /device:TPU:32 before, /device:TPU:7 now
where the time goes in v5:
time: 181 us; the launch traced here: 178 us
  waiting for transfers between devices  81.1 us (45%)
  starting transfers between devices  73.2 us (40%)
  other arithmetic  11.8 us (7%)
  matrix products  8.79 us (5%)
  local copies, waits for them, and re-layouts  2.35 us (1%)
    ppermute x8, starting transfers between devices, sent(): return lax.ppermute(value, AXES, pairs)  46.9 us
    all_to_all x2, waiting for transfers between devices, over_z(): lax.all_to_all(value, 'samp', 0, 0, tiled=True, axis_index_groups=Z_GROUPS)  37.1 us
    ppermute x8, waiting for transfers between devices, sent(): return lax.ppermute(value, AXES, pairs)  29.9 us
    all_to_all x2, starting transfers between devices, over_samp(): return lax.all_to_all(value, 'samp', 0, 0, tiled=True)  18.8 us
    all_to_all x2, waiting for transfers between devices, over_samp(): return lax.all_to_all(value, 'samp', 0, 0, tiled=True)  14 us
    dot_general x4, matrix products, tile(): lax.dot_general(scaled, panel, (((0,), (0,)), ((), ())), preferred_elemen...  8.79 us
    all_to_all x2, starting transfers between devices, over_z(): lax.all_to_all(value, 'samp', 0, 0, tiled=True, axis_index_groups=Z_GROUPS)  7.54 us
    convert_element_type x3, other arithmetic, standardized(): (observed * (observed * raw - stats[0]) * stats[1]).astype(jnp.bfloat16)  5.46 us
  transfers between devices with their start and end apart: 12, of which 7 were waited for; matrix products, arithmetic and copies ran while one was open for 11% of the time, Pallas kernels for 0%

profile of v5, /device:TPU:7, one launch (start us, length us, event | category | flops | bytes accessed | tf_op | source)
XLA Modules:
  0.0 177.5 jit_solution(6070803581309488127)
XLA Ops:
  0.0 2.7 %fusion.7 = (f32[512]{0:T(512)S(1)}, f32[512]{0:T(512)S(1)}, f32[512]{0:T(512)S(1)}) fusion(bf16[2048,512]{1,0:T(8,128)(2,1)} %param.1), kind=kLoop, calls=%fused_computation.10 | loop fusion | flops 8387072 | bytes 2103296 | tf_op jit(solution)/shard_map/reduce_sum | solution.py:91
  2.7 0.7 broadcast_in_dim.4
  3.4 11.2 %all-to-all-start = ((f32[16,3,512]{2,1,0:T(4,128)}), f32[16,3,512]{2,1,0:T(4,128)S(1)}, u32[]{:S(2)}, u32[]{:S(2)}) async-start(f32[16,3,512]{2,1,0:T(4,128)} %broadcast_in_dim.4), calls=%async_computation | async-start | bytes 262144 | tf_op jit(solution)/shard_map/all_to_all | solution.py:47
  14.6 3.1 %collective-permute-start = (bf16[2048,512]{1,0:T(8,128)(2,1)}, bf16[2048,512]{1,0:T(8,128)(2,1)}, u32[]{:S(2)}, u32[]{:S(2)}) collective-permute-start(bf16[2048,512]{1,0:T(8,128)(2,1)} %param.1), channel_id=1, source_target_pairs={{16,0},{18,2},{20,4},{22,6},{24,8},{26,10},{28,12},{30,14},{17,1},... | collective-permute-start | bytes 6291464 | tf_op jit(solution)/shard_map/ppermute | solution.py:39
  17.8 4.3 %all-to-all-done = f32[16,3,512]{2,1,0:T(4,128)S(1)} async-done(((f32[16,3,512]{2,1,0:T(4,128)}), f32[16,3,512]{2,1,0:T(4,128)S(1)}, u32[]{:S(2)}, u32[]{:S(2)}) %all-to-all-start) | async-done | bytes 98336 | tf_op jit(solution)/shard_map/all_to_all | solution.py:47
  22.1 2.5 %fusion.9 = bf16[2048,512]{1,0:T(8,128)(2,1)S(1)} fusion(bf16[2048,512]{1,0:T(8,128)(2,1)} %param.1, f32[512]{0:T(512)S(1)} %bitcast.22, f32[512]{0:T(512)S(1)} %bitcast.23), kind=kLoop, calls=%fused_computation.12 | loop fusion | flops 7340032 | bytes 4198400 | tf_op jit(solution)/shard_map/convert_element_type | solution.py:53
  24.6 0.1 slice.102
  24.7 3.0 %collective-permute-start.6 = (bf16[2048,256]{1,0:T(8,128)(2,1)S(1)}, bf16[2048,256]{1,0:T(8,128)(2,1)S(1)}, u32[]{:S(2)}, u32[]{:S(2)}) collective-permute-start(bf16[2048,256]{1,0:T(8,128)(2,1)S(1)} %slice.102), channel_id=1, source_target_pairs={{32,0},{48,16},{34,2},{50,18},{36,4},{52,20},{38,6},{54,22},{40,8}... | collective-permute-start | bytes 3145736 | tf_op jit(solution)/shard_map/ppermute | solution.py:39
  27.7 1.7 fusion.17
  29.4 1.9 %collective-permute-start.3 = (bf16[2048,256]{1,0:T(8,128)(2,1)S(1)}, bf16[2048,256]{1,0:T(8,128)(2,1)}, u32[]{:S(2)}, u32[]{:S(2)}) collective-permute-start(bf16[2048,256]{1,0:T(8,128)(2,1)S(1)} %fusion.17), channel_id=1, source_target_pairs={{32,0},{48,16},{34,2},{50,18},{36,4},{52,20},{38,6},{54,22},{40,8}... | collective-permute-start | bytes 3145736 | tf_op jit(solution)/shard_map/ppermute | solution.py:39
  31.3 22.5 %collective-permute-done.6 = bf16[2048,256]{1,0:T(8,128)(2,1)S(1)} collective-permute-done((bf16[2048,256]{1,0:T(8,128)(2,1)S(1)}, bf16[2048,256]{1,0:T(8,128)(2,1)S(1)}, u32[]{:S(2)}, u32[]{:S(2)}) %collective-permute-start.6) | collective-permute-done | bytes 1048608 | tf_op jit(solution)/shard_map/ppermute | solution.py:39
  53.8 26.1 %collective-permute-start.7 = (bf16[2048,256]{1,0:T(8,128)(2,1)S(1)}, bf16[2048,256]{1,0:T(8,128)(2,1)S(1)}, u32[]{:S(2)}, u32[]{:S(2)}) collective-permute-start(bf16[2048,256]{1,0:T(8,128)(2,1)S(1)} %collective-permute-done.6), channel_id=1, source_target_pairs={{0,16},{16,0},{2,18},{18,2},{4,20},{20,4},{6,22},{22,6},{8,24},{24... | collective-permute-start | bytes 3145736 | tf_op jit(solution)/shard_map/ppermute | solution.py:39
  80.0 1.9 %collective-permute-start.1 = (f32[2,512]{1,0:T(2,128)S(1)}, f32[2,512]{1,0:T(2,128)S(1)}, u32[]{:S(2)}, u32[]{:S(2)}) collective-permute-start(f32[2,512]{1,0:T(2,128)S(1)} %pad_maximum_fusion.3), channel_id=1, source_target_pairs={{16,0},{18,2},{20,4},{22,6},{24,8},{26,10},{28,12},{30,14},{17,1},... | collective-permute-start | bytes 12296 | tf_op jit(solution)/shard_map/ppermute | solution.py:39
  81.9 3.4 %collective-permute-done.1 = f32[2,512]{1,0:T(2,128)S(1)} collective-permute-done((f32[2,512]{1,0:T(2,128)S(1)}, f32[2,512]{1,0:T(2,128)S(1)}, u32[]{:S(2)}, u32[]{:S(2)}) %collective-permute-start.1) | collective-permute-done | bytes 4128 | tf_op jit(solution)/shard_map/ppermute | solution.py:39
  85.3 0.1 pad.21
  85.5 0.0 collective-permute-done.3
  85.5 5.8 %collective-permute-start.4 = (bf16[2048,256]{1,0:T(8,128)(2,1)}, bf16[2048,256]{1,0:T(8,128)(2,1)}, u32[]{:S(2)}, u32[]{:S(2)}) collective-permute-start(bf16[2048,256]{1,0:T(8,128)(2,1)} %collective-permute-done.3), channel_id=1, source_target_pairs={{0,16},{16,0},{2,18},{18,2},{4,20},{20,4},{6,22},{22,6},{8,24},{24... | collective-permute-start | bytes 3145736 | tf_op jit(solution)/shard_map/ppermute | solution.py:39
  91.3 0.0 collective-permute-done
  91.3 1.3 fusion.35
  92.6 0.0 collective-permute-done.7
  92.6 0.1 constant_dynamic-update-slice_fusion.1
  92.7 2.1 %fusion.26 = bf16[512,512]{1,0:T(8,128)(2,1)} fusion(bf16[2048,512]{1,0:T(8,128)(2,1)S(1)} %fusion.9, bf16[2048,512]{1,0:T(8,128)(2,1)S(1)} %constant_dynamic-update-slice_fusion.1), kind=kOutput, calls=%fused_computation.39 | convolution fusion | flops 1074266112 | bytes 4718592 | tf_op jit(solution)/shard_map/dot_general | solution.py:104
  94.8 7.6 %all-to-all-start.3 = ((bf16[16,32,512]{2,1,0:T(8,128)(2,1)}), bf16[16,32,512]{2,1,0:T(8,128)(2,1)S(1)}, u32[]{:S(2)}, u32[]{:S(2)}) async-start(bf16[16,32,512]{2,1,0:T(8,128)(2,1)} %bitcast.11), calls=%async_computation.3 | async-start | bytes 1048576 | tf_op jit(solution)/shard_map/all_to_all | solution.py:47
  102.4 1.5 fusion.14
  103.8 0.0 collective-permute-done.4
  103.8 1.3 constant_dynamic-update-slice_fusion.2
  105.1 2.7 %fusion.24 = bf16[512,640]{1,0:T(8,128)(2,1)} fusion(bf16[2048,512]{1,0:T(8,128)(2,1)S(1)} %fusion.9, bf16[2048,640]{1,0:T(8,128)(2,1)S(1)} %constant_dynamic-update-slice_fusion.2), kind=kOutput, calls=%fused_computation.34 | convolution fusion | flops 1342832640 | bytes 5373952 | tf_op jit(solution)/shard_map/dot_general | solution.py:104
  107.8 9.8 %all-to-all-done.3 = bf16[16,32,512]{2,1,0:T(8,128)(2,1)S(1)} async-done(((bf16[16,32,512]{2,1,0:T(8,128)(2,1)}), bf16[16,32,512]{2,1,0:T(8,128)(2,1)S(1)}, u32[]{:S(2)}, u32[]{:S(2)}) %all-to-all-start.3) | async-done | bytes 524320 | tf_op jit(solution)/shard_map/all_to_all | solution.py:47
  117.6 4.0 %all-to-all-start.2 = ((bf16[8,64,640]{2,1,0:T(8,128)(2,1)}), bf16[8,64,640]{2,1,0:T(8,128)(2,1)S(1)}, u32[]{:S(2)}, u32[]{:S(2)}) async-start(bf16[8,64,640]{2,1,0:T(8,128)(2,1)} %bitcast.21), calls=%async_computation.2 | async-start | bytes 1310720 | tf_op jit(solution)/shard_map/all_to_all | solution.py:43
  121.6 1.3 fusion.25
  122.9 2.7 %fusion.30 = bf16[512,384]{1,0:T(8,128)(2,1)S(1)} fusion(bf16[2048,512]{1,0:T(8,128)(2,1)S(1)} %fusion.9, bf16[2048,512]{1,0:T(8,128)(2,1)} %collective-permute-done, f32[384]{0:T(512)S(1)} %get-tuple-element.13, f32[384]{0:T(512)S(1)} %get-tuple-element.12), kind=kOutput, calls=%fused_computation.41 | convolution fusion | flops 811204608 | bytes 4066304 | tf_op jit(solution)/shard_map/dot_general | solution.py:104
  125.7 1.0 pad_maximum_fusion
  126.7 14.1 %all-to-all-done.2 = bf16[8,64,640]{2,1,0:T(8,128)(2,1)S(1)} async-done(((bf16[8,64,640]{2,1,0:T(8,128)(2,1)}), bf16[8,64,640]{2,1,0:T(8,128)(2,1)S(1)}, u32[]{:S(2)}, u32[]{:S(2)}) %all-to-all-start.2) | async-done | bytes 655392 | tf_op jit(solution)/shard_map/all_to_all | solution.py:43
  140.8 3.6 %all-to-all-start.1 = ((bf16[8,64,896]{2,1,0:T(8,128)(2,1)}), bf16[8,64,896]{2,1,0:T(8,128)(2,1)S(1)}, u32[]{:S(2)}, u32[]{:S(2)}) async-start(bf16[8,64,896]{2,1,0:T(8,128)(2,1)} %bitcast.5), calls=%async_computation.1 | async-start | bytes 1835008 | tf_op jit(solution)/shard_map/all_to_all | solution.py:43
  144.4 0.1 convert_reduce_fusion.2
  144.5 0.1 convert_reduce_fusion.1
  144.6 3.0 %collective-permute-start.5 = (f32[32,640]{1,0:T(8,128)S(1)}, f32[32,640]{1,0:T(8,128)S(1)}, u32[]{:S(2)}, u32[]{:S(2)}) collective-permute-start(f32[32,640]{1,0:T(8,128)S(1)} %constant_dynamic-slice_fusion), channel_id=1, source_target_pairs={{0,1},{16,17},{2,3},{18,19},{4,5},{20,21},{6,7},{22,23},{8,9},{24,... | collective-permute-start | bytes 245768 | tf_op jit(solution)/shard_map/ppermute | solution.py:39
  147.6 23.0 %all-to-all-done.1 = bf16[8,64,896]{2,1,0:T(8,128)(2,1)S(1)} async-done(((bf16[8,64,896]{2,1,0:T(8,128)(2,1)}), bf16[8,64,896]{2,1,0:T(8,128)(2,1)S(1)}, u32[]{:S(2)}, u32[]{:S(2)}) %all-to-all-start.1) | async-done | bytes 917536 | tf_op jit(solution)/shard_map/all_to_all | solution.py:43
  170.5 0.1 convert_reduce_fusion
  170.7 1.9 %collective-permute-start.2 = (f32[32,896]{1,0:T(8,128)S(1)}, f32[32,896]{1,0:T(8,128)S(1)}, u32[]{:S(2)}, u32[]{:S(2)}) collective-permute-start(f32[32,896]{1,0:T(8,128)S(1)} %constant_dynamic-slice_fusion.1), channel_id=1, source_target_pairs={{0,1},{16,17},{2,3},{18,19},{4,5},{20,21},{6,7},{22,23},{8,9},{24,... | collective-permute-start | bytes 344072 | tf_op jit(solution)/shard_map/ppermute | solution.py:39
  172.6 0.0 collective-permute-done.5
  172.6 4.0 %collective-permute-done.2 = f32[32,896]{1,0:T(8,128)S(1)} collective-permute-done((f32[32,896]{1,0:T(8,128)S(1)}, f32[32,896]{1,0:T(8,128)S(1)}, u32[]{:S(2)}, u32[]{:S(2)}) %collective-permute-start.2) | collective-permute-done | bytes 114720 | tf_op jit(solution)/shard_map/ppermute | solution.py:39
  176.8 0.7 select_add_fusion
  (21 shorter events, 0.2 us)
Async XLA Ops:
  3.4 18.6 %all-to-all-start = ((f32[16,3,512]{2,1,0:T(4,128)}), f32[16,3,512]{2,1,0:T(4,128)S(1)}, u32[]{:S(2)}, u32[]{:S(2)}) async-start(f32[16,3,512]{2,1,0:T(4,128)} %broadcast_in_dim.4), calls=%async_computation | async-start | bytes 262144 | tf_op jit(solution)/shard_map/all_to_all | solution.py:47
  14.6 76.7 %collective-permute-start = (bf16[2048,512]{1,0:T(8,128)(2,1)}, bf16[2048,512]{1,0:T(8,128)(2,1)}, u32[]{:S(2)}, u32[]{:S(2)}) collective-permute-start(bf16[2048,512]{1,0:T(8,128)(2,1)} %param.1), channel_id=1, source_target_pairs={{16,0},{18,2},{20,4},{22,6},{24,8},{26,10},{28,12},{30,14},{17,1},... | collective-permute-start | bytes 6291464 | tf_op jit(solution)/shard_map/ppermute | solution.py:39
  24.7 29.2 %collective-permute-start.6 = (bf16[2048,256]{1,0:T(8,128)(2,1)S(1)}, bf16[2048,256]{1,0:T(8,128)(2,1)S(1)}, u32[]{:S(2)}, u32[]{:S(2)}) collective-permute-start(bf16[2048,256]{1,0:T(8,128)(2,1)S(1)} %slice.102), channel_id=1, source_target_pairs={{32,0},{48,16},{34,2},{50,18},{36,4},{52,20},{38,6},{54,22},{40,8}... | collective-permute-start | bytes 3145736 | tf_op jit(solution)/shard_map/ppermute | solution.py:39
  29.4 56.1 %collective-permute-start.3 = (bf16[2048,256]{1,0:T(8,128)(2,1)S(1)}, bf16[2048,256]{1,0:T(8,128)(2,1)}, u32[]{:S(2)}, u32[]{:S(2)}) collective-permute-start(bf16[2048,256]{1,0:T(8,128)(2,1)S(1)} %fusion.17), channel_id=1, source_target_pairs={{32,0},{48,16},{34,2},{50,18},{36,4},{52,20},{38,6},{54,22},{40,8}... | collective-permute-start | bytes 3145736 | tf_op jit(solution)/shard_map/ppermute | solution.py:39
  53.8 38.8 %collective-permute-start.7 = (bf16[2048,256]{1,0:T(8,128)(2,1)S(1)}, bf16[2048,256]{1,0:T(8,128)(2,1)S(1)}, u32[]{:S(2)}, u32[]{:S(2)}) collective-permute-start(bf16[2048,256]{1,0:T(8,128)(2,1)S(1)} %collective-permute-done.6), channel_id=1, source_target_pairs={{0,16},{16,0},{2,18},{18,2},{4,20},{20,4},{6,22},{22,6},{8,24},{24... | collective-permute-start | bytes 3145736 | tf_op jit(solution)/shard_map/ppermute | solution.py:39
  80.0 5.3 %collective-permute-start.1 = (f32[2,512]{1,0:T(2,128)S(1)}, f32[2,512]{1,0:T(2,128)S(1)}, u32[]{:S(2)}, u32[]{:S(2)}) collective-permute-start(f32[2,512]{1,0:T(2,128)S(1)} %pad_maximum_fusion.3), channel_id=1, source_target_pairs={{16,0},{18,2},{20,4},{22,6},{24,8},{26,10},{28,12},{30,14},{17,1},... | collective-permute-start | bytes 12296 | tf_op jit(solution)/shard_map/ppermute | solution.py:39
  85.5 18.3 %collective-permute-start.4 = (bf16[2048,256]{1,0:T(8,128)(2,1)}, bf16[2048,256]{1,0:T(8,128)(2,1)}, u32[]{:S(2)}, u32[]{:S(2)}) collective-permute-start(bf16[2048,256]{1,0:T(8,128)(2,1)} %collective-permute-done.3), channel_id=1, source_target_pairs={{0,16},{16,0},{2,18},{18,2},{4,20},{20,4},{6,22},{22,6},{8,24},{24... | collective-permute-start | bytes 3145736 | tf_op jit(solution)/shard_map/ppermute | solution.py:39
  94.8 22.8 %all-to-all-start.3 = ((bf16[16,32,512]{2,1,0:T(8,128)(2,1)}), bf16[16,32,512]{2,1,0:T(8,128)(2,1)S(1)}, u32[]{:S(2)}, u32[]{:S(2)}) async-start(bf16[16,32,512]{2,1,0:T(8,128)(2,1)} %bitcast.11), calls=%async_computation.3 | async-start | bytes 1048576 | tf_op jit(solution)/shard_map/all_to_all | solution.py:47
  117.6 23.2 %all-to-all-start.2 = ((bf16[8,64,640]{2,1,0:T(8,128)(2,1)}), bf16[8,64,640]{2,1,0:T(8,128)(2,1)S(1)}, u32[]{:S(2)}, u32[]{:S(2)}) async-start(bf16[8,64,640]{2,1,0:T(8,128)(2,1)} %bitcast.21), calls=%async_computation.2 | async-start | bytes 1310720 | tf_op jit(solution)/shard_map/all_to_all | solution.py:43
  140.8 29.7 %all-to-all-start.1 = ((bf16[8,64,896]{2,1,0:T(8,128)(2,1)}), bf16[8,64,896]{2,1,0:T(8,128)(2,1)S(1)}, u32[]{:S(2)}, u32[]{:S(2)}) async-start(bf16[8,64,896]{2,1,0:T(8,128)(2,1)} %bitcast.5), calls=%async_computation.1 | async-start | bytes 1835008 | tf_op jit(solution)/shard_map/all_to_all | solution.py:43
  144.6 28.0 %collective-permute-start.5 = (f32[32,640]{1,0:T(8,128)S(1)}, f32[32,640]{1,0:T(8,128)S(1)}, u32[]{:S(2)}, u32[]{:S(2)}) collective-permute-start(f32[32,640]{1,0:T(8,128)S(1)} %constant_dynamic-slice_fusion), channel_id=1, source_target_pairs={{0,1},{16,17},{2,3},{18,19},{4,5},{20,21},{6,7},{22,23},{8,9},{24,... | collective-permute-start | bytes 245768 | tf_op jit(solution)/shard_map/ppermute | solution.py:39
  170.7 6.0 %collective-permute-start.2 = (f32[32,896]{1,0:T(8,128)S(1)}, f32[32,896]{1,0:T(8,128)S(1)}, u32[]{:S(2)}, u32[]{:S(2)}) collective-permute-start(f32[32,896]{1,0:T(8,128)S(1)} %constant_dynamic-slice_fusion.1), channel_id=1, source_target_pairs={{0,1},{16,17},{2,3},{18,19},{4,5},{20,21},{6,7},{22,23},{8,9},{24,... | collective-permute-start | bytes 344072 | tf_op jit(solution)/shard_map/ppermute | solution.py:39
